TPU v7x, 256 devices: a whole 4x4x8 slice. The times are simulated.
256 devices in a mesh: req: 32 (over x, z), mdl: 8 (over y, core).
Axes of the slice: x: 4, y: 4, z: 8, core: 2. Of those that a mesh axis runs over, the one named last changes fastest.
Arguments:
- hidden_state: bfloat16 [1024, 2880], P('req'), may hold values from -6 to 6
- cached_length_list: int32 [1024], P('req'), may hold values from 1 to 2047, as said below
- page_table: int32 [1024, 16], P('req'), may hold values from 0 to 5631, as said below
- paged_cache_store: bfloat16 [5632, 128, 1024], P('req', None, 'mdl'), may hold values from -68 to 68, as said below
- attention_gain: float32 [2880], replicated, may hold values from 0.5 to 1.5
- qkv_weight: bfloat16 [2880, 5120], P('req', 'mdl'), may hold values from -0.109375 to 0.109375
- qkv_bias: float32 [5120], P('mdl'), may hold values from -3 to 3
- sink_logit_values: float32 [64], P('mdl'), may hold values from -1 to 4
- output_weight: bfloat16 [4096, 2880], P('mdl', 'req'), may hold values from -0.25 to 0.25
- output_bias: float32 [2880], replicated, may hold values from -3 to 3
- expert_gain: float32 [2880], replicated, may hold values from 0.5 to 1.5
- router_weight: bfloat16 [2880, 32], replicated, may hold values from -0.109375 to 0.109375
- router_bias: float32 [32], replicated, may hold values from -4 to 4
- expert_routes: int32 [1024, 4], P('req'), may hold values from 0 to 31, all different within a row; in each aligned block of 32 rows (0 to 31, 32 to 63, ...) at most 8 rows name the same one
- expand_weight: bfloat16 [32, 2880, 5760], P('req', None, 'mdl'), may hold values from -0.109375 to 0.109375
- expand_bias: float32 [32, 5760], P('req', 'mdl'), may hold values from -10 to 10
- reduce_weight: bfloat16 [32, 2880, 2880], P('req', 'mdl'), may hold values from -0.109375 to 0.109375
- reduce_bias: float32 [32, 2880], replicated, may hold values from -3 to 3
Outputs:
- layer_output: bfloat16 [1024, 2880], P('req', 'mdl')
Inputs may be any that keep to these rules, and one draw needn't show every extreme that they name: `cached_length_list`: requests r and r + 1 within a block of 32 requests share an owner; about one request in eight holds between 1536 and 2047 cached positions, at most 8 of each owner's 32, and the others at most 256; some owner, and the last owner, hold exactly 8 long ones. `page_table`: the entries of request r name pages of its owner's block, pages r // 32 * 176 to that plus 176 - 1; the pages that hold cached positions differ between requests; entries past a request's last used page are to be ignored. `paged_cache_store`: keys are stored rotated at their own positions. `expert_routes`: each token names 4 different experts; of the rows of one index of req no expert is named by more than 8.
All inputs are finite; a program needn't handle non-finite values.
Results may differ from a plain program's by a relative error of at most 0.024.
Values may be sent and summed in bfloat16 or wider, within the bound.
A program may use at most 192 MiB of HBM per device.

v0:
```python
import math

import jax
import jax.numpy as jnp
from jax import lax
from jax.sharding import PartitionSpec as P

HEAD_SIZE = 64
PAGE_POSITIONS = 128
SHORT_MAX = 256
QUERY_PER_KEY = 8
SHORT_PAGES = 2


norm_epsilon = 1e-05
rope_theta = 150000.0
swiglu_limit = 7.0
swiglu_alpha = 1.702


def normalize(row_values, gain):
    value_rows = row_values.astype(jnp.float32)
    mean_square = jnp.mean(value_rows * value_rows, axis=-1, keepdims=True)
    return value_rows * lax.rsqrt(mean_square + norm_epsilon) * gain


def apply_rotation(value_rows, positions):
    half_width = value_rows.shape[-1] // 2
    exponent = jnp.arange(half_width, dtype=jnp.float32) * (2.0 / value_rows.shape[-1])
    frequency = jnp.power(rope_theta, -exponent)
    angles = positions.astype(jnp.float32)[:, None] * frequency[None, :]
    cosine = jnp.cos(angles)[:, None, :]
    sine_part = jnp.sin(angles)[:, None, :]
    first_half = value_rows[..., :half_width]
    second_half = value_rows[..., half_width:]
    return jnp.concatenate(
        [
            first_half * cosine - second_half * sine_part,
            second_half * cosine + first_half * sine_part,
        ],
        axis=-1,
    )


def head_identity(kv_heads):
    return (jnp.arange(kv_heads)[:, None] == jnp.arange(kv_heads)[None, :]).astype(jnp.float32)


def spread_queries(query_rows):
    row_count, kv_heads, group_size, head_width = query_rows.shape
    key_slot = (jnp.arange(2) == 0).astype(jnp.float32)
    turned = jnp.swapaxes(query_rows, 2, 3).astype(jnp.float32)
    spread = jnp.einsum("rhdg,kh,s->rksdhg", turned, head_identity(kv_heads), key_slot)
    return spread.astype(jnp.bfloat16).reshape(
        row_count, kv_heads * 2 * head_width, kv_heads * group_size
    )


def part_scores(query_block, table, first_position, lengths, cache_page_store, head_width):
    row_count = query_block.shape[0]
    cached_entries = cache_page_store[table].reshape(row_count, -1, cache_page_store.shape[-1])
    score_scale = 1.0 / math.sqrt(head_width)
    scores = (
        jnp.einsum("rlc,rcq->rql", cached_entries, query_block, preferred_element_type=jnp.float32)
        * score_scale
    )
    positions = first_position + jnp.arange(scores.shape[-1])
    is_live = positions[None, :] < lengths[:, None]
    scores = jnp.where(is_live[:, None, :], scores, -jnp.inf)
    return (cached_entries, scores)


def attend_cache(
    query_rows, new_keys, new_values, lengths, local_table, cache_page_store, sink_logits
):
    row_count, kv_heads, group_size, head_width = query_rows.shape
    score_scale = 1.0 / math.sqrt(head_width)
    query_block = spread_queries(query_rows)
    short_cached, short_scores = part_scores(
        query_block, local_table[:, :SHORT_PAGES], 0, lengths, cache_page_store, head_width
    )
    long_count = row_count // 4
    is_long = lengths > SHORT_MAX
    long_rows = jnp.nonzero(is_long, size=long_count, fill_value=0)[0].astype(jnp.int32)
    long_valid = jnp.arange(long_count) < jnp.sum(is_long.astype(jnp.int32))
    long_lengths = jnp.where(long_valid, lengths[long_rows], 0)
    long_cached, long_scores = part_scores(
        query_block[long_rows],
        local_table[long_rows, SHORT_PAGES:],
        SHORT_PAGES * PAGE_POSITIONS,
        long_lengths,
        cache_page_store,
        head_width,
    )
    own_score = (
        jnp.einsum(
            "rhgd,rhd->rhg", query_rows, new_keys, preferred_element_type=jnp.float32
        ).reshape(row_count, -1)
        * score_scale
    )
    largest = jnp.maximum(jnp.maximum(jnp.max(short_scores, axis=-1), own_score), sink_logits[None])
    largest = largest.at[long_rows].max(jnp.max(long_scores, axis=-1))
    long_largest = largest[long_rows]
    short_weight = jnp.exp(short_scores - largest[..., None])
    long_weight = jnp.exp(long_scores - long_largest[..., None])
    own_weight = jnp.exp(own_score - largest)
    denominator = jnp.sum(short_weight, axis=-1) + own_weight + jnp.exp(sink_logits[None] - largest)
    denominator = denominator.at[long_rows].add(jnp.sum(long_weight, axis=-1))
    long_denominator = denominator[long_rows]
    short_share = (short_weight / denominator[..., None]).astype(jnp.bfloat16)
    long_share = (long_weight / long_denominator[..., None]).astype(jnp.bfloat16)
    own_share = (own_weight / denominator).astype(jnp.bfloat16)
    wide_mixture = jnp.einsum(
        "rql,rlc->rqc", short_share, short_cached, preferred_element_type=jnp.float32
    )
    long_mixture = jnp.einsum(
        "rql,rlc->rqc", long_share, long_cached, preferred_element_type=jnp.float32
    )
    wide_mixture = wide_mixture.at[long_rows].add(long_mixture)
    wide_mixture = wide_mixture.reshape(row_count, kv_heads, group_size, kv_heads, 2, head_width)
    value_slot = (jnp.arange(2) == 1).astype(jnp.float32)
    mixture = jnp.einsum("rhgksd,hk,s->rhgd", wide_mixture, head_identity(kv_heads), value_slot)
    own_part = own_share.astype(jnp.float32).reshape(row_count, kv_heads, group_size)
    mixture = mixture + own_part[..., None] * new_values.astype(jnp.float32)[:, :, None, :]
    return mixture.astype(jnp.bfloat16).reshape(row_count, -1)


def expert_block(received, expand_local, expand_local_bias, reduce_local):
    sources, item_count, model_width = received.shape
    flattened = received.reshape(sources * item_count, model_width)
    pre_activation = (
        jnp.dot(flattened, expand_local, preferred_element_type=jnp.float32) + expand_local_bias
    )
    gate_part = jnp.minimum(pre_activation[:, 0::2], swiglu_limit)
    up_part = jnp.clip(pre_activation[:, 1::2], -swiglu_limit, swiglu_limit)
    activation = (gate_part * jax.nn.sigmoid(swiglu_alpha * gate_part) * (up_part + 1.0)).astype(
        jnp.bfloat16
    )
    return jnp.dot(activation, reduce_local, preferred_element_type=jnp.float32).reshape(
        sources, item_count, -1
    )


def shards(
    hidden_state,
    cached_length_list,
    page_table,
    paged_cache_store,
    attention_gain,
    qkv_weight,
    qkv_bias,
    sink_logit_values,
    output_weight,
    output_bias,
    expert_gain,
    router_weight,
    router_bias,
    expert_routes,
    expand_weight,
    expand_bias,
    reduce_weight,
    reduce_bias,
):
    rows_here, model_width = hidden_state.shape
    normed = normalize(hidden_state, attention_gain).astype(jnp.bfloat16)
    qkv_full, output_full = (
        lax.all_gather(qkv_weight, "req", axis=0, tiled=True),
        lax.all_gather(output_weight, "req", axis=1, tiled=True),
    )
    projected_rows = jnp.dot(normed, qkv_full, preferred_element_type=jnp.float32)
    projected_rows = (projected_rows + qkv_bias).reshape(
        rows_here, -1, QUERY_PER_KEY + 2, HEAD_SIZE
    )
    kv_heads = projected_rows.shape[1]
    query_rows = (
        apply_rotation(
            projected_rows[:, :, :QUERY_PER_KEY].reshape(
                rows_here, kv_heads * QUERY_PER_KEY, HEAD_SIZE
            ),
            cached_length_list,
        )
        .astype(jnp.bfloat16)
        .reshape(rows_here, kv_heads, QUERY_PER_KEY, HEAD_SIZE)
    )
    new_keys = apply_rotation(projected_rows[:, :, QUERY_PER_KEY], cached_length_list).astype(
        jnp.bfloat16
    )
    new_values = projected_rows[:, :, QUERY_PER_KEY + 1].astype(jnp.bfloat16)
    local_table = page_table - lax.axis_index("req") * paged_cache_store.shape[0]
    attended = attend_cache(
        query_rows,
        new_keys,
        new_values,
        cached_length_list,
        local_table,
        paged_cache_store,
        sink_logit_values,
    )
    partial_value = jnp.dot(attended, output_full, preferred_element_type=jnp.float32)
    head_total = lax.psum(partial_value.astype(jnp.bfloat16), "mdl").astype(jnp.float32)
    residual = (hidden_state.astype(jnp.float32) + head_total + output_bias).astype(jnp.bfloat16)
    expert_input = normalize(residual, expert_gain).astype(jnp.bfloat16)
    logits = jnp.dot(expert_input, router_weight, preferred_element_type=jnp.float32) + router_bias
    experts = router_weight.shape[1]
    route_count = expert_routes.shape[1]
    one_hot = expert_routes[:, :, None] == jnp.arange(experts)[None, None, :]
    chosen = jnp.sum(jnp.where(one_hot, logits[:, None, :], 0.0), axis=-1)
    gate_weights = jax.nn.softmax(chosen, axis=-1)
    capacity = max(2, 2 * rows_here * route_count // experts)
    pair_hot = one_hot.reshape(rows_here * route_count, experts).astype(jnp.int32)
    counts_before = jnp.cumsum(pair_hot, axis=0) - pair_hot
    slot_index = jnp.sum(counts_before * pair_hot, axis=1)
    target = expert_routes.reshape(-1) * capacity + slot_index
    placement = target[:, None] == jnp.arange(experts * capacity)[None, :]
    repeated = jnp.repeat(expert_input, route_count, axis=0)
    outgoing = jnp.einsum(
        "pc,pd->cd", placement.astype(jnp.bfloat16), repeated, preferred_element_type=jnp.float32
    )
    outgoing = outgoing.astype(jnp.bfloat16).reshape(experts, capacity, model_width)
    results = expert_block(
        lax.all_to_all(outgoing, "req", split_axis=0, concat_axis=0, tiled=True),
        expand_weight[0],
        expand_bias[0],
        reduce_weight[0],
    )
    share_width = model_width // lax.axis_size("mdl")
    offset = lax.axis_index("mdl") * share_width
    shares = lax.psum_scatter(
        results.astype(jnp.bfloat16), "mdl", scatter_dimension=2, tiled=True
    ).astype(jnp.float32)
    returned = lax.all_to_all(
        shares.astype(jnp.bfloat16), "req", split_axis=0, concat_axis=0, tiled=True
    ).astype(shares.dtype)
    picked = returned.reshape(-1, share_width)[target]
    blended = jnp.sum(
        picked.reshape(rows_here, route_count, share_width) * gate_weights[:, :, None], axis=1
    )
    bias_rows = lax.dynamic_slice_in_dim(reduce_bias, offset, share_width, 1)
    bias_term = jnp.sum(bias_rows[expert_routes] * gate_weights[:, :, None], axis=1)
    residual_share = lax.dynamic_slice_in_dim(residual, offset, share_width, 1).astype(jnp.float32)
    return (residual_share + blended + bias_term).astype(jnp.bfloat16)


def solution(mesh):
    in_specs = (
        P("req", None),
        P("req"),
        P("req", None),
        P("req", None, "mdl"),
        P(),
        P("req", "mdl"),
        P("mdl"),
        P("mdl"),
        P("mdl", "req"),
        P(),
        P(),
        P(),
        P(),
        P("req", None),
        P("req", None, "mdl"),
        P("req", "mdl"),
        P("req", "mdl", None),
        P(),
    )
    out_specs = P("req", "mdl")
    return jax.shard_map(shards, mesh=mesh, in_specs=in_specs, out_specs=out_specs, check_vma=False)
```

profile of v0, /device:TPU:1, one launch (start us, length us, event | category | flops | bytes accessed | tf_op | source)
XLA Modules:
  0.0 449.0 jit_solution(11918151416933086248)
XLA Ops:
  6.5 0.7 all-gather.7.cloned.1.call-update
  7.3 0.7 all-gather.5.cloned.1.call-update
  8.1 0.7 broadcast_subtract_fusion
  9.0 0.7 fusion.55
  9.9 0.8 scatter_custom_fusion
  10.9 1.4 fusion.56
  12.2 0.7 fusion.79
  12.9 1.3 gather_fusion.1
  14.2 0.7 compare_select_fusion.5
  14.9 16.5 %while.1 = (s32[]{:T(128)}, s32[32,16]{0,1:T(8,128)S(1)}, s32[8,2]{0,1:T(2,128)S(1)}, s32[8,14]{1,0:T(8,128)S(1)}, s32[]{:T(128)}, /*index=5*/s32[]{:T(128)}) while((s32[]{:T(128)}, s32[32,16]{0,1:T(8,128)S(1)}, s32[8,2]{0,1:T(2,128)S(1)}, s32[8,14]{1,0:T(8,128)S(1)}, s32[]{:T(128)}, /*index=5*/s32[]{:T(128)}) %tuple.28), condition=%wide.while_cond, body=%wide.while_body.sunk | while | flops 2 | bytes 449 | solution.py:89
  15.0 0.5 fusion.81
  15.5 1.3 dynamic-slice.7
  17.0 0.5 fusion.81
  17.6 1.3 dynamic-slice.7
  19.6 1.3 dynamic-slice.7
  21.7 1.3 dynamic-slice.7
  23.8 1.3 dynamic-slice.7
  25.8 1.3 dynamic-slice.7
  27.4 0.5 fusion.81
  27.9 1.3 dynamic-slice.7
  29.4 0.5 fusion.81
  30.0 1.3 dynamic-slice.7
  31.5 4.8 %gather_fusion = bf16[64,128,128]{2,1,0:T(8,128)(2,1)} fusion(bf16[176,128,128]{2,1,0:T(8,128)(2,1)} %param.21, s32[1024]{0:T(1024)S(1)} %pad_clamp_fusion.4), kind=kCustom, calls=%fused_computation | custom fusion | bytes 4194560 | tf_op jit(solution)/shard_map/gather | solution.py:61
  36.4 5.7 %gather_fusion.3 = bf16[112,128,128]{2,1,0:T(8,128)(2,1)} fusion(bf16[176,128,128]{2,1,0:T(8,128)(2,1)} %param.21, s32[1024]{0:T(1024)S(1)} %pad_clamp_fusion.2), kind=kCustom, calls=%fused_computation.3 | custom fusion | bytes 7340480 | tf_op jit(solution)/shard_map/gather | solution.py:61
  42.9 0.7 compare_select_fusion.8
  43.8 45.9 %all-gather.7.cloned.1.call-done = bf16[32,90,512]{2,1,0:T(8,128)(2,1)} async-done(((bf16[1,90,512]{2,1,0:T(8,128)(2,1)}), bf16[32,90,512]{2,1,0:T(8,128)(2,1)}) %all-gather.7.cloned.1.call-update) | async-done | bytes 2949136 | tf_op jit(solution)/shard_map/all_gather | solution.py:168
  89.7 4.4 reshape.625
  94.1 77.2 %all-gather.5.cloned.1.call-done = bf16[32,90,640]{2,1,0:T(8,128)(2,1)} async-done(((bf16[1,90,640]{2,1,0:T(8,128)(2,1)}), bf16[32,90,640]{2,1,0:T(8,128)(2,1)}) %all-gather.5.cloned.1.call-update) | async-done | bytes 3686416 | tf_op jit(solution)/shard_map/all_gather | solution.py:167
  171.4 4.9 %reshape.623 = bf16[2880,640]{1,0:T(8,128)(2,1)} reshape(bf16[32,90,640]{2,1,0:T(8,128)(2,1)} %all-gather.5.cloned.1.call-done) | data formatting | bytes 7372800
  176.2 2.8 convolution_add_fusion
  180.2 0.6 gather_fusion.2
  180.7 2.3 fusion.64
  183.1 3.2 fusion.65
  186.3 0.6 scatter_fusion
  186.9 0.6 gather_fusion.4
  187.9 0.6 scatter_fusion.1
  188.5 0.6 gather_fusion.5
  189.1 2.0 fusion.29
  191.2 2.7 fusion.21
  193.9 0.8 scatter_fusion.2
  195.3 3.5 convolution_convert_fusion.2
  198.8 62.6 %all-reduce.3.cloned.1.call-done = bf16[32,2880]{1,0:T(8,128)(2,1)} async-done(((bf16[32,2880]{1,0:T(8,128)(2,1)}), bf16[32,2880]{1,0:T(8,128)(2,1)}) %all-reduce.3.cloned.1.call-update) | async-done | bytes 184336 | tf_op jit(solution)/shard_map/psum | solution.py:200
  261.4 1.1 fusion.12
  262.6 1.1 broadcast_in_dim.57
  263.7 1.6 reshape.490
  265.3 1.8 convolution_convert_fusion.1
  267.0 2.6 copy.49
  269.6 9.4 %all-to-all-start = ((bf16[32,8,2880]{2,1,0:T(8,128)(2,1)}), bf16[32,8,2880]{2,1,0:T(8,128)(2,1)}, u32[]{:S(2)}, u32[]{:S(2)}) async-start(bf16[32,8,2880]{2,1,0:T(8,128)(2,1)} %bitcast.100), calls=%async_computation | async-start | bytes 3014656 | tf_op jit(solution)/shard_map/all_to_all | solution.py:221
  279.3 32.1 %all-to-all-done = bf16[32,8,2880]{2,1,0:T(8,128)(2,1)} async-done(((bf16[32,8,2880]{2,1,0:T(8,128)(2,1)}), bf16[32,8,2880]{2,1,0:T(8,128)(2,1)}, u32[]{:S(2)}, u32[]{:S(2)}) %all-to-all-start) | async-done | bytes 1474592 | tf_op jit(solution)/shard_map/all_to_all | solution.py:221
  311.4 4.9 %fusion.5 = f32[256,720]{0,1:T(8,128)} fusion(bf16[1,2880,720]{1,2,0:T(8,128)(2,1)} %param.32, bf16[32,8,2880]{2,1,0:T(8,128)(2,1)} %all-to-all-done, f32[720]{0:T(1024)S(1)} %reduce.1), kind=kOutput, calls=%fused_computation.22 | convolution fusion | flops 1061867520 | bytes 6361920 | tf_op jit(solution)/shard_map/dot_general | solution.py:132
  316.3 2.1 slice.39
  318.3 2.1 slice.40
  320.8 2.1 convolution_convert_fusion
  322.8 20.3 %copy.58 = bf16[32,8,2880]{1,0,2:T(8,128)(2,1)} copy(bf16[32,8,2880]{2,1,0:T(8,128)(2,1)} %convolution_convert_fusion) | data formatting | bytes 2949120
  343.2 32.7 %reshape.631 = bf16[2880,256]{1,0:T(8,128)(2,1)} reshape(bf16[2880,32,8]{2,1,0:T(8,128)(2,1)} %bitcast.94) | data formatting | bytes 2949120
  376.4 0.9 constant_dynamic-slice_fusion.1
  377.3 0.8 gather_fusion.7
  378.4 33.7 %reduce-scatter.4.cloned.1.call-done = bf16[360,256]{1,0:T(8,128)(2,1)} async-done(((bf16[2880,256]{1,0:T(8,128)(2,1)}), bf16[360,256]{1,0:T(8,128)(2,1)}) %reduce-scatter.4.cloned.1.call-update) | async-done | bytes 184336
  412.1 5.4 %reshape.632 = bf16[360,32,8]{2,1,0:T(8,128)(2,1)} reshape(bf16[360,256]{1,0:T(8,128)(2,1)} %reduce-scatter.4.cloned.1.call-done) | data formatting | bytes 368640
  417.5 4.5 copy.59
  422.0 9.2 %all-to-all-start.1 = ((bf16[32,8,360]{2,1,0:T(8,128)(2,1)}), bf16[32,8,360]{2,1,0:T(8,128)(2,1)S(1)}, u32[]{:S(2)}, u32[]{:S(2)}) async-start(bf16[32,8,360]{2,1,0:T(8,128)(2,1)} %copy.59), calls=%async_computation.1 | async-start | bytes 393216 | tf_op jit(solution)/shard_map/all_to_all | solution.py:231
  431.5 9.1 %all-to-all-done.1 = bf16[32,8,360]{2,1,0:T(8,128)(2,1)S(1)} async-done(((bf16[32,8,360]{2,1,0:T(8,128)(2,1)}), bf16[32,8,360]{2,1,0:T(8,128)(2,1)S(1)}, u32[]{:S(2)}, u32[]{:S(2)}) %all-to-all-start.1) | async-done | bytes 184352 | tf_op jit(solution)/shard_map/all_to_all | solution.py:231
  440.7 0.8 gather_fusion.6
  441.8 0.7 add_convert_fusion.2
  (132 shorter events, 9.9 us)
Async XLA Ops:
  6.5 314.2 %copy-start = (bf16[1,360,2880]{2,1,0:T(8,128)(2,1)S(1)}, bf16[1,360,2880]{2,1,0:T(8,128)(2,1)}, u32[]{:S(2)}) copy-start(bf16[1,360,2880]{2,1,0:T(8,128)(2,1)} %param.34) | copy-start | bytes 6220804
  6.5 83.2 %all-gather.7.cloned.1.call-start = ((), (), s32[]{:S(2)}) async-start(), calls=%async_computation.5 | async-start | bytes 3244032 | tf_op jit(solution)/shard_map/all_gather | solution.py:168
  7.3 164.1 %all-gather.5.cloned.1.call-start = ((), (), s32[]{:S(2)}) async-start(), calls=%async_computation.4 | async-start | bytes 4055040 | tf_op jit(solution)/shard_map/all_gather | solution.py:167
  8.0 253.4 %all-reduce.3.cloned.1.call-start = ((), (), s32[]{:S(2)}) async-start(), calls=%async_computation.3 | async-start | bytes 376832 | tf_op jit(solution)/shard_map/psum | solution.py:200
  36.3 5.7 %copy-start.5 = (s32[32,4]{0,1:T(4,128)S(1)}, s32[32,4]{0,1:T(4,128)}, u32[]{:S(2)}) copy-start(s32[32,4]{0,1:T(4,128)} %param.31) | copy-start | bytes 1540
  36.3 6.4 %copy-start.3 = (bf16[32,2880]{1,0:T(8,128)(2,1)S(1)}, bf16[32,2880]{1,0:T(8,128)(2,1)}, u32[]{:S(2)}) copy-start(bf16[32,2880]{1,0:T(8,128)(2,1)} %param.18) | copy-start | bytes 552964
  36.3 7.2 %copy-start.2 = (s32[32]{0:T(128)S(1)}, s32[32]{0:T(128)}, u32[]{:S(2)}) copy-start(s32[32]{0:T(128)} %param.19) | copy-start | bytes 388
  94.1 82.1 %copy-start.8 = (f32[2880]{0:T(1024)S(1)}, f32[2880]{0:T(1024)}, u32[]{:S(2)}) copy-start(f32[2880]{0:T(1024)} %param.22) | copy-start | bytes 34564
  94.1 82.1 %copy-start.9 = (f32[640]{0:T(1024)S(1)}, f32[640]{0:T(1024)}, u32[]{:S(2)}) copy-start(f32[640]{0:T(1024)} %param.24) | copy-start | bytes 7684
  179.1 4.0 copy-start.11
  193.9 67.5 %copy-start.7 = (f32[2880]{0:T(1024)S(1)}, f32[2880]{0:T(1024)}, u32[]{:S(2)}) copy-start(f32[2880]{0:T(1024)} %param.27) | copy-start | bytes 34564
  193.9 68.6 %copy-start.6 = (f32[2880]{0:T(1024)S(1)}, f32[2880]{0:T(1024)}, u32[]{:S(2)}) copy-start(f32[2880]{0:T(1024)} %param.28) | copy-start | bytes 34564
  267.0 12.2 %copy-start.10 = (f32[1,720]{1,0:T(1,128)S(1)}, f32[1,720]{1,0:T(1,128)}, u32[]{:S(2)}) copy-start(f32[1,720]{1,0:T(1,128)} %param.33) | copy-start | bytes 8644
  269.6 41.8 %all-to-all-start = ((bf16[32,8,2880]{2,1,0:T(8,128)(2,1)}), bf16[32,8,2880]{2,1,0:T(8,128)(2,1)}, u32[]{:S(2)}, u32[]{:S(2)}) async-start(bf16[32,8,2880]{2,1,0:T(8,128)(2,1)} %bitcast.100), calls=%async_computation | async-start | bytes 3014656 | tf_op jit(solution)/shard_map/all_to_all | solution.py:221
  279.0 133.1 %reduce-scatter.4.cloned.1.call-start = ((), (), s32[]{:S(2)}) async-start(), calls=%async_computation.6 | async-start | bytes 1658880
  375.9 2.2 copy-start.4
  375.9 2.2 copy-start.12
  417.5 25.0 %copy-start.1 = (bf16[1,360,2880]{2,1,0:T(8,128)(2,1)S(1)}, bf16[1,360,2880]{2,1,0:T(8,128)(2,1)}, u32[]{:S(2)}) copy-start(bf16[1,360,2880]{2,1,0:T(8,128)(2,1)} %param.34) | copy-start | bytes 6220804
  422.0 18.7 %all-to-all-start.1 = ((bf16[32,8,360]{2,1,0:T(8,128)(2,1)}), bf16[32,8,360]{2,1,0:T(8,128)(2,1)S(1)}, u32[]{:S(2)}, u32[]{:S(2)}) async-start(bf16[32,8,360]{2,1,0:T(8,128)(2,1)} %copy.59), calls=%async_computation.1 | async-start | bytes 393216 | tf_op jit(solution)/shard_map/all_to_all | solution.py:231
Sparse Core Ops, SparseCore 0:
  9.9 79.7 all-gather.6
  92.3 79.0 all-gather.4
  198.9 62.4 all-reduce.2
  376.1 35.9 reduce-scatter.3
where the time goes:
time: 454 us; the launch traced here: 449 us
  waiting for transfers between devices  262 us (58%)
  local copies, waits for them, and re-layouts  116 us (26%)
  matrix products  25.9 us (6%)
  starting transfers between devices  19 us (4%)
  between operations  13.7 us (3%)
  other arithmetic  12.7 us (3%)
    all_gather x1, waiting for transfers between devices, shards(): lax.all_gather(qkv_weight, 'req', axis=0, tiled=True)  77.2 us
    unnamed x33, local copies, waits for them, and re-layouts  72.4 us
    psum x1, waiting for transfers between devices, shards(): lax.psum(partial_value.astype(jnp.bfloat16), 'mdl').astype(jnp.float32)  62.6 us
    all_gather x1, waiting for transfers between devices, shards(): lax.all_gather(output_weight, 'req', axis=1, tiled=True)  45.9 us
    unnamed x5, waiting for transfers between devices  35.1 us
    all_to_all x1, waiting for transfers between devices, shards(): lax.all_to_all(outgoing, 'req', split_axis=0, concat_axis=0, tiled=True)  32.1 us
    gather x40, local copies, waits for them, and re-layouts  16.5 us
    gather x2, local copies, waits for them, and re-layouts, part_scores(): cache_page_store[table].reshape(row_count, -1, cache_page_store.shape[-1])  10.5 us
  transfers between devices with their start and end apart: 6, of which 6 were waited for; matrix products, arithmetic and copies ran while one was open for 9% of the time, Pallas kernels for 0%

commit v1 on v0

v1 whole, which is shorter than its diff:
```python
import functools
import math

import jax
import jax.numpy as jnp
from jax import lax
from jax.experimental import pallas as pl
from jax.experimental.pallas import tpu as pltpu
from jax.sharding import PartitionSpec as P

HEAD_SIZE = 64
PAGE_POSITIONS = 128
SHORT_MAX = 256
QUERY_PER_KEY = 8
SHORT_PAGES = 2
SLOTS = 8

NX, NZ, NY, NC = 4, 8, 4, 2

norm_epsilon = 1e-05
rope_theta = 150000.0
swiglu_limit = 7.0
swiglu_alpha = 1.702

BF = jnp.bfloat16
F32 = jnp.float32
VMEM_LIMIT = 58 * 2**20
MESH = pl.DeviceIdType.MESH


def place():
    r = lax.axis_index("req")
    m = lax.axis_index("mdl")
    return r, m, r // NZ, r % NZ, m // NC, m % NC


def device(r, m):
    return {"req": r, "mdl": m}


def dot(a, b):
    return jnp.dot(a, b, preferred_element_type=F32)


def dot_nt(a, b):
    return lax.dot_general(a, b, (((1,), (1,)), ((), ())), preferred_element_type=F32)


def split3(value):
    high = value.astype(BF)
    rest = value - high.astype(F32)
    middle = rest.astype(BF)
    low = (rest - middle.astype(F32)).astype(BF)
    return high, middle, low


class Ring:
    def __init__(self, size, me, ref_of, send, recv, target):
        self.size, self.me, self.ref_of = size, me, ref_of
        self.send, self.recv, self.target = send, recv, target
        self.half = size // 2
        self.plan = [
            (way, dist, part)
            for dist in range(1, self.half + 1)
            for part in range(2)
            for way in range(2)
            if self.exists(way, dist, part)
        ]

    def exists(self, way, dist, part):
        return dist < self.half or (dist == self.half and part == way)

    def index(self, way, dist, part):
        return (way * self.half + dist - 1) * 2 + part

    def origin(self, way, dist):
        return (self.me + (dist if way else self.size - dist)) % self.size

    def copy(self, way, dist, part):
        ref = self.ref_of(self.origin(way, dist - 1), part)
        i = self.index(way, dist, part)
        to = (self.me + (self.size - 1 if way else 1)) % self.size
        return pltpu.make_async_remote_copy(
            src_ref=ref,
            dst_ref=ref,
            send_sem=self.send.at[i],
            recv_sem=self.recv.at[i],
            device_id=self.target(to),
            device_id_type=MESH,
        )

    def arrive(self, way, dist, part):
        ref = self.ref_of(self.origin(way, dist), part)
        i = self.index(way, dist, part)
        pltpu.make_async_remote_copy(
            src_ref=ref,
            dst_ref=ref,
            send_sem=self.send.at[i],
            recv_sem=self.recv.at[i],
            device_id=self.target(self.me),
            device_id_type=MESH,
        ).wait_recv()

    def begin(self, part):
        for way in range(2):
            if self.exists(way, 1, part):
                self.copy(way, 1, part).start()

    def step(self, way, dist, part):
        self.arrive(way, dist, part)
        if self.exists(way, dist + 1, part):
            self.copy(way, dist + 1, part).start()

    def finish(self):
        for way, dist, part in self.plan:
            self.copy(way, dist, part).wait_send()


def remote(src, dst, send, recv, r, m):
    return pltpu.make_async_remote_copy(
        src_ref=src,
        dst_ref=dst,
        send_sem=send,
        recv_sem=recv,
        device_id=device(r, m),
        device_id_type=MESH,
    )


def ring_sems(size):
    return [pltpu.SemaphoreType.DMA((2 * size,)), pltpu.SemaphoreType.DMA((2 * size,))]


def lane_cut(width):
    tiles = width // 128
    return 128 * ((tiles + 1) // 2) if tiles > 1 else 0


def project_kernel(
    hidden, gain, wqkv, wo, bias,
    proj, wo_out,
    gathered, wo_all, parcels, rows, blocks, total, sums, sums_in,
    ring_send, ring_recv, wo_send, wo_recv, x_send, x_recv, s_send, s_recv, local,
):
    r, m, x, z, y, c = place()
    tokens, width = hidden.shape
    group = width // NX
    block = group // NZ

    load_q = pltpu.make_async_copy(wqkv, gathered.at[z], local.at[0])
    load_o = pltpu.make_async_copy(wo, wo_all.at[z], local.at[1])
    load_q.start()
    load_o.start()

    barrier = pltpu.get_barrier_semaphore()
    for step in (1, NZ - 1):
        pl.semaphore_signal(barrier, inc=1, device_id=device(x * NZ + (z + step) % NZ, m), device_id_type=MESH)
    for step in range(1, NX):
        pl.semaphore_signal(barrier, inc=1, device_id=device((x + step) % NX * NZ + z, m), device_id_type=MESH)
    load_q.wait()
    pl.semaphore_wait(barrier, NX + 1)

    cut_q, cut_o = lane_cut(wqkv.shape[1]), lane_cut(wo.shape[1])

    def part_of(buffer, cut):
        full = buffer.shape[-1]

        def ref_of(origin, part):
            return buffer.at[origin, :, pl.ds(0, cut) if part == 0 else pl.ds(cut, full - cut)]

        return ref_of

    def at_z(to):
        return device(x * NZ + to, m)

    ring = Ring(NZ, z, part_of(gathered, cut_q), ring_send, ring_recv, at_z)
    ring_o = Ring(NZ, z, part_of(wo_all, cut_o), wo_send, wo_recv, at_z)
    for part in range(2):
        ring.begin(part)

    value = hidden[...].astype(F32)
    scale = lax.rsqrt(jnp.mean(value * value, axis=-1, keepdims=True) + norm_epsilon)
    normed = (value * scale * gain[...]).astype(BF)
    for k in range(NX):
        parcels[k] = normed[:, group * k : group * k + group]

    def x_copy(src, dst, send, recv, step):
        to = (x + step) % NX
        return remote(src.at[to], dst.at[x], send.at[step], recv.at[step], to * NZ + z, m)

    def x_arrive(dst, send, recv, step):
        origin = (x + NX - step) % NX
        remote(dst.at[origin], dst.at[origin], send.at[step], recv.at[step], r, m).wait_recv()

    for step in range(1, NX):
        x_copy(parcels, rows, x_send, x_recv, step).start()
    rows[x] = parcels[x]

    for step in range(1, NX):
        x_arrive(rows, x_send, x_recv, step)
    for k in range(NZ):
        for j in range(NX):
            blocks[k, j * tokens : (j + 1) * tokens] = rows[j, :, block * k : block * k + block]

    def add(origin, first):
        product = dot(blocks[origin], gathered[origin])
        for j in range(NX):
            piece = product[j * tokens : (j + 1) * tokens]
            total[j] = piece if first else total[j] + piece

    add(z, True)
    for dist in range(1, ring.half + 1):
        for way, d, part in ring.plan:
            if d == dist:
                ring.step(way, d, part)
        if dist == ring.half - 1 or ring.half == 1:
            load_o.wait()
            for part in range(2):
                ring_o.begin(part)
        add(ring.origin(0, dist), False)
        if dist < ring.half:
            add(ring.origin(1, dist), False)

    for j in range(NX):
        sums[j] = total[j].astype(BF)
    for step in range(1, NX):
        x_copy(sums, sums_in, s_send, s_recv, step).start()
    for way, dist, part in ring_o.plan:
        ring_o.step(way, dist, part)
    result = total[x] + bias[...]
    for step in range(1, NX):
        x_arrive(sums_in, s_send, s_recv, step)
        result = result + sums_in[(x + NX - step) % NX].astype(F32)
    proj[...] = result
    for k in range(NZ):
        wo_out[k] = wo_all[k]

    ring.finish()
    ring_o.finish()
    for step in range(1, NX):
        x_copy(parcels, rows, x_send, x_recv, step).wait_send()
        x_copy(sums, sums_in, s_send, s_recv, step).wait_send()


def project(hidden, gain, wqkv, wo, bias):
    tokens, width = hidden.shape
    group = width // NX
    block, cols = wqkv.shape
    out_rows = wo.shape[1]
    vmem = pl.BlockSpec(memory_space=pltpu.VMEM)
    hbm = pl.BlockSpec(memory_space=pl.ANY)
    return pl.pallas_call(
        project_kernel,
        name="project",
        out_shape=(
            jax.ShapeDtypeStruct((tokens, cols), F32),
            jax.ShapeDtypeStruct((NZ, block, out_rows), BF),
        ),
        in_specs=[vmem, vmem, hbm, hbm, vmem],
        out_specs=(vmem, vmem),
        scratch_shapes=[
            pltpu.VMEM((NZ, block, cols), BF),
            pltpu.VMEM((NZ, block, out_rows), BF),
            pltpu.VMEM((NX, tokens, group), BF),
            pltpu.VMEM((NX, tokens, group), BF),
            pltpu.VMEM((NZ, NX * tokens, block), BF),
            pltpu.VMEM((NX, tokens, cols), F32),
            pltpu.VMEM((NX, tokens, cols), BF),
            pltpu.VMEM((NX, tokens, cols), BF),
            *ring_sems(NZ),
            *ring_sems(NZ),
            *[pltpu.SemaphoreType.DMA((NX,))] * 4,
            pltpu.SemaphoreType.DMA((2,)),
        ],
        compiler_params=pltpu.CompilerParams(
            collective_id=1, has_side_effects=True, vmem_limit_bytes=VMEM_LIMIT
        ),
    )(hidden, gain, wqkv, wo, bias)


def attend_kernel(
    lengths, table, proj, cosines, sines, sinks, cache,
    out,
    short, long, queries, mixed, owns, short_sem, long_sem,
):
    count = proj.shape[0]
    heads = QUERY_PER_KEY
    pages = table.shape[1]
    score_scale = 1.0 / math.sqrt(HEAD_SIZE)

    def fetch(i, used):
        for p in range(SHORT_PAGES):
            pltpu.make_async_copy(
                cache.at[table[i, p]], short.at[i, pl.ds(p * PAGE_POSITIONS, PAGE_POSITIONS)], short_sem.at[i]
            ).start()
        is_long = lengths[i] > SHORT_MAX

        @pl.when(is_long)
        def _():
            for p in range(SHORT_PAGES, pages):
                pltpu.make_async_copy(
                    cache.at[table[i, p]],
                    long.at[used, pl.ds((p - SHORT_PAGES) * PAGE_POSITIONS, PAGE_POSITIONS)],
                    long_sem.at[used],
                ).start()

        return used + is_long.astype(jnp.int32)

    lax.fori_loop(0, count, fetch, jnp.int32(0))

    value = proj[...]
    lanes = lax.broadcasted_iota(jnp.int32, value.shape, 1)
    width = value.shape[1]
    first = (lanes % HEAD_SIZE) < HEAD_SIZE // 2
    partner = jnp.where(
        first,
        pltpu.roll(value, width - HEAD_SIZE // 2, axis=1),
        pltpu.roll(value, HEAD_SIZE // 2, axis=1),
    )
    repeat = width // cosines.shape[1]
    turned = value * jnp.concatenate([cosines[...]] * repeat, axis=1) + partner * jnp.concatenate(
        [sines[...]] * repeat, axis=1
    )
    key_at = heads * HEAD_SIZE
    rounded = jnp.where(lanes < key_at + HEAD_SIZE, turned, value).astype(BF).astype(F32)
    new_key = rounded[:, key_at : key_at + HEAD_SIZE]
    new_value = rounded[:, key_at + HEAD_SIZE :]
    queries[...] = jnp.zeros_like(queries)
    for h in range(heads):
        head = rounded[:, h * HEAD_SIZE : (h + 1) * HEAD_SIZE]
        queries[:, h, 0:HEAD_SIZE] = head
        own = jnp.sum(head * new_key, axis=1, keepdims=True) * score_scale
        owns[:, h, :] = jnp.broadcast_to(own, (count, owns.shape[2]))
    sink = sinks[...]

    def one(i, used):
        length = lengths[i]
        query = queries[i].astype(BF)
        own = owns[i][:, 0:1]
        pltpu.make_async_copy(short.at[i], short.at[i], short_sem.at[i]).wait()
        entries = short[i]
        scores = dot_nt(query, entries) * score_scale
        positions = lax.broadcasted_iota(jnp.int32, scores.shape, 1)
        scores = jnp.where(positions < length, scores, -jnp.inf)
        largest = jnp.maximum(jnp.maximum(jnp.max(scores, axis=1, keepdims=True), own), sink)
        is_long = length > SHORT_MAX

        @pl.when(jnp.logical_not(is_long))
        def _():
            weight = jnp.exp(scores - largest)
            own_weight = jnp.exp(own - largest)
            bottom = jnp.sum(weight, axis=1, keepdims=True) + own_weight + jnp.exp(sink - largest)
            mixed[i] = dot((weight / bottom).astype(BF), entries)
            owns[i] = jnp.broadcast_to((own_weight / bottom).astype(BF).astype(F32), owns.shape[1:])

        @pl.when(is_long)
        def _():
            pltpu.make_async_copy(long.at[used], long.at[used], long_sem.at[used]).wait()
            far = long[used]
            more = dot_nt(query, far) * score_scale
            at = lax.broadcasted_iota(jnp.int32, more.shape, 1) + SHORT_MAX
            more = jnp.where(at < length, more, -jnp.inf)
            top = jnp.maximum(largest, jnp.max(more, axis=1, keepdims=True))
            weight = jnp.exp(scores - top)
            far_weight = jnp.exp(more - top)
            own_weight = jnp.exp(own - top)
            bottom = (
                jnp.sum(weight, axis=1, keepdims=True)
                + jnp.sum(far_weight, axis=1, keepdims=True)
                + own_weight
                + jnp.exp(sink - top)
            )
            mixed[i] = dot((weight / bottom).astype(BF), entries) + dot((far_weight / bottom).astype(BF), far)
            owns[i] = jnp.broadcast_to((own_weight / bottom).astype(BF).astype(F32), owns.shape[1:])

        return used + is_long.astype(jnp.int32)

    lax.fori_loop(0, count, one, jnp.int32(0))
    for h in range(heads):
        head = mixed[:, h, HEAD_SIZE:] + owns[:, h, 0:1] * new_value
        out[:, h * HEAD_SIZE : (h + 1) * HEAD_SIZE] = head.astype(BF)


def attend(lengths, table, proj, cosines, sines, sinks, cache):
    count = proj.shape[0]
    channels = cache.shape[2]
    pages = table.shape[1]
    vmem = pl.BlockSpec(memory_space=pltpu.VMEM)
    smem = pl.BlockSpec(memory_space=pltpu.SMEM)
    most_long = count // 4
    return pl.pallas_call(
        attend_kernel,
        name="attend",
        out_shape=jax.ShapeDtypeStruct((count, QUERY_PER_KEY * HEAD_SIZE), BF),
        in_specs=[smem, smem, vmem, vmem, vmem, vmem, pl.BlockSpec(memory_space=pl.ANY)],
        out_specs=vmem,
        scratch_shapes=[
            pltpu.VMEM((count, SHORT_PAGES * PAGE_POSITIONS, channels), BF),
            pltpu.VMEM((most_long, (pages - SHORT_PAGES) * PAGE_POSITIONS, channels), BF),
            pltpu.VMEM((count, QUERY_PER_KEY, channels), F32),
            pltpu.VMEM((count, QUERY_PER_KEY, channels), F32),
            pltpu.VMEM((count, QUERY_PER_KEY, channels), F32),
            pltpu.SemaphoreType.DMA((count,)),
            pltpu.SemaphoreType.DMA((most_long,)),
        ],
        compiler_params=pltpu.CompilerParams(vmem_limit_bytes=VMEM_LIMIT),
    )(lengths, table, proj, cosines, sines, sinks, cache)


def expert_kernel(
    att, wo_all, hidden, obias, egain, router, router_bias, routes, routes_t, w1_hbm, b1, w2_hbm, rbias,
    out,
    w1, w2, heads, halves, summed, mine, outgoing, gathered, full, pre, near_out, near_in, far_out, far_in,
    kept, back_out, back_in, logits_out, logits_in, share_f32, gains,
    x_send, x_recv, s_send, s_recv, d_send, d_recv, ring_send, ring_recv, p_send, p_recv,
    n_send, n_recv, f_send, f_recv, b_send, b_recv, l_send, l_recv, local,
):
    r, m, x, z, y, c = place()
    tokens, width = hidden.shape
    count_req, count_mdl = NX * NZ, NY * NC
    share = width // count_mdl
    block = width // count_req
    padded = outgoing.shape[2]
    rows = count_req * SLOTS
    per_group = NZ * block // share

    load1 = pltpu.make_async_copy(w1_hbm, w1, local.at[0])
    load2 = pltpu.make_async_copy(w2_hbm, w2, local.at[1])
    load1.start()
    load2.start()

    barrier = pltpu.get_barrier_semaphore()

    def greet(to_r, to_m):
        pl.semaphore_signal(barrier, inc=1, device_id=device(to_r, to_m), device_id_type=MESH)

    def greet_req(step, carry):
        greet((r + step) % count_req, m)
        return carry

    lax.fori_loop(1, count_req, greet_req, 0)
    for step in range(1, count_mdl):
        greet(r, (m + step) % count_mdl)
    diagonal = x == y
    for step in range(NX):
        for j in range(per_group):
            not_me = jnp.logical_or(step > 0, per_group * x + j != m)

            @pl.when(not_me)
            def _():
                greet((x + step) % NX * NZ + z, per_group * x + j)

    for j in range(count_mdl):

        @pl.when(jnp.logical_not(jnp.logical_and(diagonal, m == j)))
        def _():
            greet(y * NZ + z, j)

    pl.semaphore_wait(
        barrier,
        (count_req - 1) + (count_mdl - 1) + NX * per_group + count_mdl - 2 * diagonal.astype(jnp.int32),
    )

    for step in range(1, NX):
        to = (x + step) % NX
        remote(att, heads.at[x], x_send.at[step], x_recv.at[step], to * NZ + z, m).start()
    heads[x] = att[...]

    for k in range(count_mdl):

        @pl.when(m == k)
        def _():
            at = slice(share * k, share * k + share)
            share_f32[...] = hidden[:, at].astype(F32) + obias[:, at]
            gains[0:1, :] = egain[:, at]
            gains[8 : 8 + count_req, :] = rbias[:, at]
            gains[8 + count_req : 8 + 2 * count_req, :] = router[:, at].astype(F32)

    names = lax.broadcasted_iota(jnp.int32, (count_req, tokens), 0)
    hot_t = jnp.zeros((count_req, tokens), F32)
    for k in range(routes_t.shape[0]):
        hot_t = hot_t + (routes_t[k : k + 1, :] == names).astype(F32)
    names = lax.broadcasted_iota(jnp.int32, (tokens, count_req), 1)
    hot = jnp.zeros((tokens, count_req), F32)
    for k in range(routes.shape[1]):
        hot = hot + (routes[:, k : k + 1] == names).astype(F32)
    before = lax.broadcasted_iota(jnp.int32, (tokens, tokens), 0) < lax.broadcasted_iota(
        jnp.int32, (tokens, tokens), 1
    )
    rank_t = dot(hot_t.astype(BF), before.astype(BF))
    after = lax.broadcasted_iota(jnp.int32, (tokens, tokens), 0) > lax.broadcasted_iota(
        jnp.int32, (tokens, tokens), 1
    )
    rank = dot(after.astype(BF), hot.astype(BF))
    spread = (
        lax.broadcasted_iota(jnp.int32, (rows, count_req), 0) // SLOTS
        == lax.broadcasted_iota(jnp.int32, (rows, count_req), 1)
    ).astype(BF)
    spread_t = (
        lax.broadcasted_iota(jnp.int32, (count_req, rows), 1) // SLOTS
        == lax.broadcasted_iota(jnp.int32, (count_req, rows), 0)
    ).astype(BF)
    slot = (lax.broadcasted_iota(jnp.int32, (rows, tokens), 0) % SLOTS).astype(F32)
    place_rows = jnp.where(
        jnp.logical_and(dot(spread, hot_t.astype(BF)) > 0.5, dot(spread, rank_t.astype(BF)) == slot), 1.0, 0.0
    ).astype(BF)
    slot_t = (lax.broadcasted_iota(jnp.int32, (tokens, rows), 1) % SLOTS).astype(F32)
    take_rows = jnp.where(
        jnp.logical_and(dot(hot.astype(BF), spread_t) > 0.5, dot(rank.astype(BF), spread_t) == slot_t), 1.0, 0.0
    )

    for step in range(1, NX):
        origin = (x + NX - step) % NX
        remote(heads.at[origin], heads.at[origin], x_send.at[step], x_recv.at[step], r, m).wait_recv()

    stacked = jnp.concatenate([heads[j] for j in range(NX)], axis=0)
    per_share = share // block
    for k in range(NZ):
        product = dot_nt(stacked, wo_all[k]).astype(BF)
        for j in range(NX):
            halves[k // per_share, j, :, block * (k % per_share) : block * (k % per_share) + block] = product[
                j * tokens : (j + 1) * tokens
            ]

    def sum_copy(step, j):
        to = (x + step) % NX
        i = step * per_group + j
        return remote(
            halves.at[j, to], summed.at[m], s_send.at[i], s_recv.at[m], to * NZ + z, per_group * x + j
        )

    for step in range(NX):
        for j in range(per_group):

            @pl.when(jnp.logical_or(step > 0, per_group * x + j != m))
            def _():
                sum_copy(step, j).start()

    @pl.when(diagonal)
    def _():
        summed[m] = halves[m % per_group, x]

    residual = share_f32[...]
    for j in range(count_mdl):

        @pl.when(jnp.logical_not(jnp.logical_and(diagonal, m == j)))
        def _():
            remote(summed.at[j], summed.at[j], s_send.at[0], s_recv.at[j], r, m).wait_recv()

    total = summed[0].astype(F32)
    for j in range(1, count_mdl):
        total = total + summed[j].astype(F32)
    residual = (residual + total).astype(BF).astype(F32)
    share_f32[...] = residual
    squares = jnp.sum(residual * residual, axis=1, keepdims=True)
    scaled = (residual * gains[0:1, :]).astype(BF)
    mine[...] = jnp.zeros_like(mine)
    mine[:, 0:share] = scaled
    for k, piece in enumerate(split3(squares)):
        mine[:, share + k : share + k + 1] = piece

    outgoing[...] = dot(place_rows, mine[...]).astype(BF).reshape(outgoing.shape)

    def send_row(step, carry):
        to = (r + step) % count_req
        remote(outgoing.at[to], gathered.at[m, r], d_send.at[step], d_recv.at[r], to, m).start()
        return carry

    lax.fori_loop(1, count_req, send_row, 0)
    gathered[m, r] = outgoing[r]

    routing = gains[8 + count_req : 8 + 2 * count_req, :].astype(BF)
    logits_out[...] = jnp.zeros_like(logits_out)
    logits_out[:, 0:count_req] = dot_nt(scaled, routing)
    logits_out[:, count_req : count_req + 1] = squares
    for step in range(1, count_mdl):
        to = (m + step) % count_mdl
        remote(logits_out, logits_in.at[m], l_send.at[step], l_recv.at[step], r, to).start()
    logits_in[m] = logits_out[...]

    part_rows = count_req // 2

    def part_ref(origin, part):
        return gathered.at[origin * NC + c, pl.ds(part * part_rows, part_rows)]

    def at_y(to):
        return device(r, to * NC + c)

    ring = Ring(NY, y, part_ref, ring_send, ring_recv, at_y)

    def pair_index(way, dist):
        return way * ring.half + dist

    def pair_copy(way, dist, part):
        origin = ring.origin(way, dist)
        ref = part_ref(origin, part)
        i = pair_index(way, dist) * 2 + part
        return remote(ref, ref, p_send.at[i], p_recv.at[i], r, y * NC + 1 - c)

    def pair_arrive(way, dist, part):
        ref = gathered.at[ring.origin(way, dist) * NC + 1 - c, pl.ds(part * part_rows, part_rows)]
        i = pair_index(way, dist) * 2 + part
        remote(ref, ref, p_send.at[i], p_recv.at[i], r, m).wait_recv()

    for part in range(2):

        def take(origin, carry):
            @pl.when(origin != r)
            def _():
                remote(gathered.at[m, origin], gathered.at[m, origin], d_send.at[0], d_recv.at[origin], r, m).wait_recv()

            return carry

        lax.fori_loop(part * part_rows, (part + 1) * part_rows, take, 0)
        ring.begin(part)
        pair_copy(0, 0, part).start()

    for way, dist, part in ring.plan:
        ring.step(way, dist, part)
        pair_copy(way, dist, part).start()
    pair_plan = [(0, 0, 0), (0, 0, 1)] + ring.plan
    for way, dist, part in pair_plan:
        pair_arrive(way, dist, part)

    load1.wait()
    load2.wait()
    square_sum = jnp.zeros((rows, 1), F32)
    for k in range(count_mdl):
        piece = gathered[k].reshape(rows, padded)
        full[:, share * k : share * k + share] = piece[:, 0:share]
        for j in range(3):
            square_sum = square_sum + piece[:, share + j : share + j + 1].astype(F32)
    root = lax.rsqrt(square_sum * (1.0 / width) + norm_epsilon)
    columns = w1.shape[0]
    pre[...] = jnp.zeros_like(pre)
    pre[:, 0:columns] = dot_nt(full[...], w1[...]) * root + b1[...]
    raw = pre[...]
    up = jnp.clip(pltpu.roll(raw, raw.shape[1] - 1, axis=1), -swiglu_limit, swiglu_limit)
    gate = jnp.minimum(raw, swiglu_limit)
    act = (gate * jax.nn.sigmoid(swiglu_alpha * gate) * (up + 1.0)).astype(BF)
    hidden_units = columns // 2
    pick = (
        lax.broadcasted_iota(jnp.int32, (raw.shape[1], hidden_units), 0)
        == 2 * lax.broadcasted_iota(jnp.int32, (raw.shape[1], hidden_units), 1)
    ).astype(BF)
    act = dot(act, pick).astype(BF)

    def produce(k):
        return dot(act, w2[:, share * k : share * k + share])

    def near_copy(k):
        return remote(near_out.at[k], near_in.at[k], n_send.at[k], n_recv.at[k], r, y * NC + 1 - c)

    for core in range(NC):

        @pl.when(c == core)
        def _():
            for k in range(NY):
                near_out[k] = produce(k * NC + 1 - core).astype(BF)
                near_copy(k).start()
            for k in range(NY):
                kept[k] = produce(k * NC + core)

    def far_copy(step):
        to = (y + step) % NY
        return remote(far_out.at[to], far_in.at[y], f_send.at[step], f_recv.at[step], r, to * NC + c)

    for step in range(1, NY):
        to = (y + step) % NY
        remote(near_in.at[to], near_in.at[to], n_send.at[to], n_recv.at[to], r, m).wait_recv()
        far_out[to] = (kept[to] + near_in[to].astype(F32)).astype(BF)
        far_copy(step).start()
    remote(near_in.at[y], near_in.at[y], n_send.at[y], n_recv.at[y], r, m).wait_recv()
    answer = kept[y] + near_in[y].astype(F32)
    for step in range(1, NY):
        origin = (y + NY - step) % NY
        remote(far_in.at[origin], far_in.at[origin], f_send.at[step], f_recv.at[step], r, m).wait_recv()
        answer = answer + far_in[origin].astype(F32)
    back_out[...] = answer.astype(BF).reshape(back_out.shape)

    def send_back(step, carry):
        to = (r + step) % count_req
        remote(back_out.at[to], back_in.at[r], b_send.at[step], b_recv.at[step], to, m).start()
        return carry

    lax.fori_loop(1, count_req, send_back, 0)
    back_in[r] = back_out[r]

    for step in range(1, count_mdl):
        origin = (m + count_mdl - step) % count_mdl
        remote(logits_in.at[origin], logits_in.at[origin], l_send.at[step], l_recv.at[step], r, m).wait_recv()
    both = logits_in[0]
    for k in range(1, count_mdl):
        both = both + logits_in[k]
    row_root = lax.rsqrt(both[:, count_req : count_req + 1] * (1.0 / width) + norm_epsilon)
    logits = both[:, 0:count_req] * row_root + router_bias[...]
    logits = jnp.where(hot > 0.5, logits, -jnp.inf)
    weight = jnp.exp(logits - jnp.max(logits, axis=1, keepdims=True))
    gates = weight / jnp.sum(weight, axis=1, keepdims=True)
    result = share_f32[...]
    biases = split3(gains[8 : 8 + count_req, :])
    gate_parts = split3(gates)
    for i in range(3):
        for j in range(3 - i):
            result = result + dot(gate_parts[i], biases[j])
    takers = [(take_rows * dot(piece, spread_t)).astype(BF) for piece in gate_parts]

    def take_back(step, carry):
        origin = (r + count_req - step) % count_req
        remote(back_in.at[origin], back_in.at[origin], b_send.at[step], b_recv.at[step], r, m).wait_recv()
        return carry

    lax.fori_loop(1, count_req, take_back, 0)
    returned = back_in[...].reshape(rows, share)
    for taker in takers:
        result = result + dot(taker, returned)
    out[...] = result.astype(BF)

    for step in range(1, NX):
        to = (x + step) % NX
        remote(att, heads.at[x], x_send.at[step], x_recv.at[step], to * NZ + z, m).wait_send()
    for step in range(NX):
        for j in range(per_group):

            @pl.when(jnp.logical_or(step > 0, per_group * x + j != m))
            def _():
                sum_copy(step, j).wait_send()

    def sent(step, carry):
        to = (r + step) % count_req
        remote(outgoing.at[to], gathered.at[m, r], d_send.at[step], d_recv.at[r], to, m).wait_send()
        remote(back_out.at[to], back_in.at[r], b_send.at[step], b_recv.at[step], to, m).wait_send()
        return carry

    lax.fori_loop(1, count_req, sent, 0)
    ring.finish()
    for way, dist, part in pair_plan:
        pair_copy(way, dist, part).wait_send()
    for k in range(NY):
        near_copy(k).wait_send()
    for step in range(1, NY):
        far_copy(step).wait_send()
    for step in range(1, count_mdl):
        to = (m + step) % count_mdl
        remote(logits_out, logits_in.at[m], l_send.at[step], l_recv.at[step], r, to).wait_send()


def experts(att, wo_all, hidden, obias, egain, router, router_bias, routes, routes_t, w1, b1, w2, rbias):
    tokens, width = hidden.shape
    count_req, count_mdl = NX * NZ, NY * NC
    share = width // count_mdl
    padded = -(-(share + 3) // 128) * 128
    rows = count_req * SLOTS
    columns = w1.shape[0]
    wide = -(-(columns + 1) // 128) * 128
    per_group = count_mdl // NX
    vmem = pl.BlockSpec(memory_space=pltpu.VMEM)
    hbm = pl.BlockSpec(memory_space=pl.ANY)
    dma = pltpu.SemaphoreType.DMA
    return pl.pallas_call(
        expert_kernel,
        name="experts",
        out_shape=jax.ShapeDtypeStruct((tokens, share), BF),
        in_specs=[vmem] * 9 + [hbm, vmem, hbm, vmem],
        out_specs=vmem,
        scratch_shapes=[
            pltpu.VMEM(w1.shape, BF),
            pltpu.VMEM(w2.shape, BF),
            pltpu.VMEM((NX,) + att.shape, BF),
            pltpu.VMEM((per_group, NX, tokens, share), BF),
            pltpu.VMEM((count_mdl, tokens, share), BF),
            pltpu.VMEM((tokens, padded), BF),
            pltpu.VMEM((count_req, SLOTS, padded), BF),
            pltpu.VMEM((count_mdl, count_req, SLOTS, padded), BF),
            pltpu.VMEM((rows, width), BF),
            pltpu.VMEM((rows, wide), F32),
            pltpu.VMEM((NY, rows, share), BF),
            pltpu.VMEM((NY, rows, share), BF),
            pltpu.VMEM((NY, rows, share), BF),
            pltpu.VMEM((NY, rows, share), BF),
            pltpu.VMEM((NY, rows, share), F32),
            pltpu.VMEM((count_req, SLOTS, share), BF),
            pltpu.VMEM((count_req, SLOTS, share), BF),
            pltpu.VMEM((tokens, 128), F32),
            pltpu.VMEM((count_mdl, tokens, 128), F32),
            pltpu.VMEM((tokens, share), F32),
            pltpu.VMEM((8 + 2 * count_req, share), F32),
            dma((NX,)), dma((NX,)),
            dma((NX * per_group,)), dma((count_mdl,)),
            dma((count_req,)), dma((count_req,)),
            *ring_sems(NY),
            dma((2 * (NY + 2),)), dma((2 * (NY + 2),)),
            dma((NY,)), dma((NY,)),
            dma((NY,)), dma((NY,)),
            dma((count_req,)), dma((count_req,)),
            dma((count_mdl,)), dma((count_mdl,)),
            dma((2,)),
        ],
        compiler_params=pltpu.CompilerParams(
            collective_id=2, has_side_effects=True, vmem_limit_bytes=VMEM_LIMIT
        ),
    )(att, wo_all, hidden, obias, egain, router, router_bias, routes, routes_t, w1, b1, w2, rbias)


def rotation_tables(lengths, repeat):
    half = HEAD_SIZE // 2
    exponent = jnp.arange(half, dtype=F32) * (2.0 / HEAD_SIZE)
    frequency = jnp.power(rope_theta, -exponent)
    angles = lengths.astype(F32)[:, None] * frequency[None, :]
    cosine, sine = jnp.cos(angles), jnp.sin(angles)
    return (
        jnp.concatenate([cosine, cosine] * repeat, axis=1),
        jnp.concatenate([-sine, sine] * repeat, axis=1),
    )


def shards(
    hidden_state,
    cached_length_list,
    page_table,
    paged_cache_store,
    attention_gain,
    qkv_weight,
    qkv_bias,
    sink_logit_values,
    output_weight,
    output_bias,
    expert_gain,
    router_weight,
    router_bias,
    expert_routes,
    expand_weight,
    expand_bias,
    reduce_weight,
    reduce_bias,
):
    projected, wo_all = project(
        hidden_state, attention_gain[None], qkv_weight, output_weight.T, qkv_bias[None]
    )
    pool = paged_cache_store.shape[0]
    local_table = jnp.clip(page_table - lax.axis_index("req") * pool, 0, pool - 1)
    cosines, sines = rotation_tables(cached_length_list, 2)
    attended = attend(
        cached_length_list, local_table, projected, cosines, sines, sink_logit_values[:, None], paged_cache_store
    )
    return experts(
        attended,
        wo_all,
        hidden_state,
        output_bias[None],
        expert_gain[None],
        router_weight.T,
        router_bias[None],
        expert_routes,
        expert_routes.T,
        expand_weight[0].T,
        expand_bias,
        reduce_weight[0],
        reduce_bias,
    )


def solution(mesh):
    in_specs = (
        P("req", None),
        P("req"),
        P("req", None),
        P("req", None, "mdl"),
        P(),
        P("req", "mdl"),
        P("mdl"),
        P("mdl"),
        P("mdl", "req"),
        P(),
        P(),
        P(),
        P(),
        P("req", None),
        P("req", None, "mdl"),
        P("req", "mdl"),
        P("req", "mdl", None),
        P(),
    )
    out_specs = P("req", "mdl")
    return jax.shard_map(shards, mesh=mesh, in_specs=in_specs, out_specs=out_specs, check_vma=False)
```

time: 454 us -> 139 us (0.31)
  waiting for transfers between devices: 262 us -> 0 us
  Pallas kernels: 0 us -> 128 us
  local copies, waits for them, and re-layouts: 116 us -> 7.94 us
  matrix products: 25.9 us -> 0 us
  starting transfers between devices: 19 us -> 0 us
  between operations: 13.7 us -> 0.05 us
  other arithmetic: 12.7 us -> 2.18 us
    pallas_call x0 -> x3, Pallas kernels: none -> 128 us  [the longest x1 68.8 us: experts(): pl.pallas_call(expert_kernel, name='experts', out_shape=jax.ShapeDtypeStr...]
    all_gather x2 -> x0, waiting for transfers between devices: 123 us -> none  [the longest x1 77.2 us: shards(): lax.all_gather(qkv_weight, 'req', axis=0, tiled=True)]
    unnamed x33 -> x9, local copies, waits for them, and re-layouts: 72.4 us -> 2.82 us
    psum x1 -> x0, waiting for transfers between devices: 62.6 us -> none  [shards(): lax.psum(partial_value.astype(jnp.bfloat16), 'mdl').astype(jnp.float32)]
    all_to_all x2 -> x0, waiting for transfers between devices: 41.2 us -> none  [the longest x1 32.1 us: shards(): lax.all_to_all(outgoing, 'req', split_axis=0, concat_axis=0, tiled=True)]
    unnamed x5 -> x0, waiting for transfers between devices: 35.1 us -> none
    gather x49 -> x0, local copies, waits for them, and re-layouts: 31.5 us -> none
    dot_general x12 -> x0, matrix products: 25.9 us -> none  [the longest x2 5.49 us: part_scores(): jnp.einsum('rlc,rcq->rql', cached_entries, query_block, preferred_element...]
  transfers between devices with their start and end apart: 6 -> 0, of which waited for: 6 -> 0; matrix products, arithmetic and copies ran while one was open for 9% -> 0% of each run, Pallas kernels for 0% -> 0%
where the time goes in v1:
time: 139 us; the launch traced here: 138 us
  Pallas kernels  128 us (92%)
  local copies, waits for them, and re-layouts  7.94 us (6%)
  other arithmetic  2.18 us (2%)
    pallas_call x1, Pallas kernels, experts(): pl.pallas_call(expert_kernel, name='experts', out_shape=jax.ShapeDtypeStr...  68.8 us
    pallas_call x1, Pallas kernels, project(): pl.pallas_call(project_kernel, name='project', out_shape=(jax.ShapeDtypeS...  33.3 us
    pallas_call x1, Pallas kernels, attend(): pl.pallas_call(attend_kernel, name='attend', out_shape=jax.ShapeDtypeStru...  26.1 us
    unnamed x9, local copies, waits for them, and re-layouts  2.82 us

profile of v1, /device:TPU:1, one launch (start us, length us, event | category | flops | bytes accessed | tf_op | source)
XLA Modules:
  0.0 138.4 jit_solution(7932183422703182425)
XLA Ops:
  0.0 0.0 copy-start.2
  0.0 0.0 copy-start
  0.0 0.0 copy-start.1
  0.0 0.7 convert_element_type.3
  0.7 0.1 fusion
  0.9 0.7 pad_maximum_fusion
  1.6 1.3 broadcast_in_dim.20.gain
  2.9 1.3 broadcast_in_dim.21.bias
  4.2 33.3 %project.1 = (f32[32,640]{1,0:T(8,128)}, bf16[8,90,512]{2,1,0:T(8,128)(2,1)}) custom-call(bf16[32,2880]{1,0:T(8,128)(2,1)} %hidden.3, f32[1,2880]{1,0:T(1,128)} %broadcast_in_dim.20.gain, bf16[90,640]{1,0:T(8,128)(2,1)} %wqkv.1, bf16[90,512]{1,0:T(8,128)(2,1)} %bitcast.12, f32[1,640]{1,0:T(1,128)} %broadcast_in_dim.21.bias), custom_call_target="tpu_custom_call" | custom-call | tf_op jit(solution)/shard_map/project/pallas_call | solution.py:252
  37.5 0.8 copy.22
  38.3 0.6 subtract_clamp_fusion.table
  38.9 1.3 copy.24.sinks
  40.2 26.1 %attend.1.att = bf16[32,512]{1,0:T(8,128)(2,1)} custom-call(s32[32]{0:T(128)} %lengths.1, s32[32,16]{1,0:T(8,128)} %subtract_clamp_fusion.table, f32[32,640]{1,0:T(8,128)} %get-tuple-element.7.proj, f32[32,128]{1,0:T(8,128)} %get-tuple-element.12.cosines, f32[32,128]{1,0:T(8,128)} %get-tuple-element.13.sines, f32[8,1]{1,0:T(8,128)} %copy.24.sinks, ...), custom_call_target="tpu_custom_call" | custom-call | tf_op jit(solution)/shard_map/attend/pallas_call | solution.py:391
  66.3 0.0 copy-done.2
  66.3 0.7 copy.25.routes
  67.0 0.0 copy-done
  67.0 0.6 broadcast_in_dim.23.obias
  67.6 0.0 copy-done.1
  67.6 0.6 broadcast_in_dim.24.egain
  68.2 68.8 %experts.1 = bf16[32,360]{1,0:T(8,128)(2,1)} custom-call(bf16[32,512]{1,0:T(8,128)(2,1)} %attend.1.att, bf16[8,90,512]{2,1,0:T(8,128)(2,1)} %get-tuple-element.8.wo_all, bf16[32,2880]{1,0:T(8,128)(2,1)} %hidden.3, f32[1,2880]{1,0:T(1,128)} %broadcast_in_dim.23.obias, f32[1,2880]{1,0:T(1,128)} %broadcast_in_dim.24.egain, bf16[32,2880]{1,0:T(8,128)(2,1)} %bitcast.11, ...), custom_call_target="tpu_custom_call" | custom-call | tf_op jit(solution)/shard_map/experts/pallas_call | solution.py:760
  137.1 1.3 copy.27
  (1 shorter events, 0.0 us)
Async XLA Ops:
  0.0 66.3 %copy-start.2 = (s32[32,4]{0,1:T(4,128)S(1)}, s32[32,4]{0,1:T(4,128)}, u32[]{:S(2)}) copy-start(s32[32,4]{0,1:T(4,128)} %param.31) | copy-start | bytes 1540
  0.0 67.0 %copy-start = (f32[2880]{0:T(1024)S(1)}, f32[2880]{0:T(1024)}, u32[]{:S(2)}) copy-start(f32[2880]{0:T(1024)} %param.27) | copy-start | bytes 34564
  0.0 67.6 %copy-start.1 = (f32[2880]{0:T(1024)S(1)}, f32[2880]{0:T(1024)}, u32[]{:S(2)}) copy-start(f32[2880]{0:T(1024)} %param.28) | copy-start | bytes 34564

commit v2 on v1

--- a/solution.py
+++ b/solution.py
@@ -25,6 +25,7 @@
 BF = jnp.bfloat16
 F32 = jnp.float32
 VMEM_LIMIT = 58 * 2**20
+LOWEST = -1e30
 MESH = pl.DeviceIdType.MESH
 
 
@@ -278,35 +279,36 @@
     )(hidden, gain, wqkv, wo, bias)
 
 
+def find_long(lengths, count, most_long, rank, at_long):
+    def see(i, carry):
+        seen, places = carry
+        rank[i] = jnp.minimum(seen, most_long - 1)
+        seen = seen + (lengths[i] > SHORT_MAX).astype(jnp.int32)
+        return seen, tuple(p + (seen <= j).astype(jnp.int32) for j, p in enumerate(places))
+
+    zero = jnp.int32(0)
+    _, places = lax.fori_loop(0, count, see, (zero, (zero,) * most_long))
+    for j in range(most_long):
+        at_long[j] = jnp.minimum(places[j], count - 1)
+
+
 def attend_kernel(
     lengths, table, proj, cosines, sines, sinks, cache,
     out,
-    short, long, queries, mixed, owns, short_sem, long_sem,
+    pool, rank, at_long, scores, far_scores, queries, owns, tops, bottoms, mixed,
+    far_top, far_bottom, far_mixed, load,
 ):
+    r = lax.axis_index("req")
+    load_pool = pltpu.make_async_copy(cache, pool, load.at[0])
+    load_pool.start()
     count = proj.shape[0]
     heads = QUERY_PER_KEY
-    pages = table.shape[1]
+    most_long = far_scores.shape[0]
+    find_long(lengths, count, most_long, rank, at_long)
+    pages = table.shape[0]
+    channels = pool.shape[2]
     score_scale = 1.0 / math.sqrt(HEAD_SIZE)
-
-    def fetch(i, used):
-        for p in range(SHORT_PAGES):
-            pltpu.make_async_copy(
-                cache.at[table[i, p]], short.at[i, pl.ds(p * PAGE_POSITIONS, PAGE_POSITIONS)], short_sem.at[i]
-            ).start()
-        is_long = lengths[i] > SHORT_MAX
-
-        @pl.when(is_long)
-        def _():
-            for p in range(SHORT_PAGES, pages):
-                pltpu.make_async_copy(
-                    cache.at[table[i, p]],
-                    long.at[used, pl.ds((p - SHORT_PAGES) * PAGE_POSITIONS, PAGE_POSITIONS)],
-                    long_sem.at[used],
-                ).start()
-
-        return used + is_long.astype(jnp.int32)
-
-    lax.fori_loop(0, count, fetch, jnp.int32(0))
+    base = r * pool.shape[0]
 
     value = proj[...]
     lanes = lax.broadcasted_iota(jnp.int32, value.shape, 1)
@@ -330,85 +332,121 @@
         head = rounded[:, h * HEAD_SIZE : (h + 1) * HEAD_SIZE]
         queries[:, h, 0:HEAD_SIZE] = head
         own = jnp.sum(head * new_key, axis=1, keepdims=True) * score_scale
-        owns[:, h, :] = jnp.broadcast_to(own, (count, owns.shape[2]))
-    sink = sinks[...]
-
-    def one(i, used):
-        length = lengths[i]
-        query = queries[i].astype(BF)
-        own = owns[i][:, 0:1]
-        pltpu.make_async_copy(short.at[i], short.at[i], short_sem.at[i]).wait()
-        entries = short[i]
-        scores = dot_nt(query, entries) * score_scale
-        positions = lax.broadcasted_iota(jnp.int32, scores.shape, 1)
-        scores = jnp.where(positions < length, scores, -jnp.inf)
-        largest = jnp.maximum(jnp.maximum(jnp.max(scores, axis=1, keepdims=True), own), sink)
-        is_long = length > SHORT_MAX
-
-        @pl.when(jnp.logical_not(is_long))
-        def _():
-            weight = jnp.exp(scores - largest)
-            own_weight = jnp.exp(own - largest)
-            bottom = jnp.sum(weight, axis=1, keepdims=True) + own_weight + jnp.exp(sink - largest)
-            mixed[i] = dot((weight / bottom).astype(BF), entries)
-            owns[i] = jnp.broadcast_to((own_weight / bottom).astype(BF).astype(F32), owns.shape[1:])
-
-        @pl.when(is_long)
-        def _():
-            pltpu.make_async_copy(long.at[used], long.at[used], long_sem.at[used]).wait()
-            far = long[used]
-            more = dot_nt(query, far) * score_scale
-            at = lax.broadcasted_iota(jnp.int32, more.shape, 1) + SHORT_MAX
-            more = jnp.where(at < length, more, -jnp.inf)
-            top = jnp.maximum(largest, jnp.max(more, axis=1, keepdims=True))
-            weight = jnp.exp(scores - top)
-            far_weight = jnp.exp(more - top)
+        owns[:, h, :] = jnp.broadcast_to(own, (count, channels))
+    load_pool.wait()
+
+    def entries(i, start, stop):
+        return jnp.concatenate(
+            [pool[jnp.clip(table[p, i] - base, 0, pool.shape[0] - 1)] for p in range(start, stop)], axis=0
+        )
+
+    def masked(raw, i, start):
+        positions = lax.broadcasted_iota(jnp.int32, raw.shape, 1) + start
+        return jnp.where(positions < lengths[i], raw * score_scale, LOWEST)
+
+    at_once = 8 if count % 8 == 0 else 1
+
+    def score(g, carry):
+        for u in range(at_once):
+            i = g * at_once + u
+            scores[i] = masked(dot_nt(queries[i].astype(BF), entries(i, 0, SHORT_PAGES)), i, 0)
+        return carry
+
+    lax.fori_loop(0, count // at_once, score, 0)
+
+    def far_score(j, carry):
+        i = at_long[j]
+        far_scores[j] = masked(dot_nt(queries[i].astype(BF), entries(i, SHORT_PAGES, pages)), i, SHORT_MAX)
+        return carry
+
+    lax.fori_loop(0, most_long, far_score, 0)
+
+    def weigh(held, tops, bottoms):
+        raw = held[...]
+        top = jnp.max(raw, axis=2, keepdims=True)
+        weight = jnp.exp(raw - top)
+        held[...] = weight
+        tops[...] = jnp.broadcast_to(top, tops.shape)
+        bottoms[...] = jnp.broadcast_to(jnp.sum(weight, axis=2, keepdims=True), bottoms.shape)
+
+    weigh(scores, tops, bottoms)
+    weigh(far_scores, far_top, far_bottom)
+
+    def mix(g, carry):
+        for u in range(at_once):
+            i = g * at_once + u
+            mixed[i] = dot(scores[i].astype(BF), entries(i, 0, SHORT_PAGES))
+        return carry
+
+    lax.fori_loop(0, count // at_once, mix, 0)
+
+    def far_mix(j, carry):
+        far_mixed[j] = dot(far_scores[j].astype(BF), entries(at_long[j], SHORT_PAGES, pages))
+        return carry
+
+    lax.fori_loop(0, most_long, far_mix, 0)
+
+    sink_rows = lax.broadcasted_iota(jnp.int32, (heads, channels), 0)
+    sink = jnp.zeros((heads, channels), F32)
+    for h in range(heads):
+        sink = jnp.where(sink_rows == h, sinks[h], sink)
+
+    def join(g, carry):
+        for u in range(at_once):
+            i = g * at_once + u
+            k = rank[i]
+            is_long = jnp.full((heads, channels), lengths[i], jnp.int32) > SHORT_MAX
+            far = jnp.where(is_long, far_top[k], LOWEST)
+            own = owns[i]
+            near = tops[i]
+            top = jnp.maximum(jnp.maximum(near, far), jnp.maximum(own, sink))
+            near_scale = jnp.exp(near - top)
+            far_scale = jnp.exp(far - top)
             own_weight = jnp.exp(own - top)
-            bottom = (
-                jnp.sum(weight, axis=1, keepdims=True)
-                + jnp.sum(far_weight, axis=1, keepdims=True)
-                + own_weight
-                + jnp.exp(sink - top)
-            )
-            mixed[i] = dot((weight / bottom).astype(BF), entries) + dot((far_weight / bottom).astype(BF), far)
-            owns[i] = jnp.broadcast_to((own_weight / bottom).astype(BF).astype(F32), owns.shape[1:])
-
-        return used + is_long.astype(jnp.int32)
-
-    lax.fori_loop(0, count, one, jnp.int32(0))
+            bottom = bottoms[i] * near_scale + own_weight + jnp.exp(sink - top)
+            bottom = bottom + jnp.where(is_long, far_bottom[k] * far_scale, 0.0)
+            both = mixed[i] * near_scale + jnp.where(is_long, far_mixed[k] * far_scale, 0.0)
+            mixed[i] = both / bottom
+            owns[i] = own_weight / bottom
+        return carry
+
+    lax.fori_loop(0, count // at_once, join, 0)
     for h in range(heads):
         head = mixed[:, h, HEAD_SIZE:] + owns[:, h, 0:1] * new_value
         out[:, h * HEAD_SIZE : (h + 1) * HEAD_SIZE] = head.astype(BF)
 
 
 def attend(lengths, table, proj, cosines, sines, sinks, cache):
-    count = proj.shape[0]
+    tokens = proj.shape[0]
     channels = cache.shape[2]
-    pages = table.shape[1]
+    pages = table.shape[0]
+    most_long = tokens // 4
     vmem = pl.BlockSpec(memory_space=pltpu.VMEM)
     smem = pl.BlockSpec(memory_space=pltpu.SMEM)
-    most_long = count // 4
+    per_head = pltpu.VMEM((tokens, QUERY_PER_KEY, channels), F32)
+    per_long = pltpu.VMEM((most_long, QUERY_PER_KEY, channels), F32)
     return pl.pallas_call(
         attend_kernel,
         name="attend",
-        out_shape=jax.ShapeDtypeStruct((count, QUERY_PER_KEY * HEAD_SIZE), BF),
-        in_specs=[smem, smem, vmem, vmem, vmem, vmem, pl.BlockSpec(memory_space=pl.ANY)],
+        out_shape=jax.ShapeDtypeStruct((tokens, QUERY_PER_KEY * HEAD_SIZE), BF),
+        in_specs=[smem, smem, vmem, vmem, vmem, smem, pl.BlockSpec(memory_space=pl.ANY)],
         out_specs=vmem,
         scratch_shapes=[
-            pltpu.VMEM((count, SHORT_PAGES * PAGE_POSITIONS, channels), BF),
-            pltpu.VMEM((most_long, (pages - SHORT_PAGES) * PAGE_POSITIONS, channels), BF),
-            pltpu.VMEM((count, QUERY_PER_KEY, channels), F32),
-            pltpu.VMEM((count, QUERY_PER_KEY, channels), F32),
-            pltpu.VMEM((count, QUERY_PER_KEY, channels), F32),
-            pltpu.SemaphoreType.DMA((count,)),
-            pltpu.SemaphoreType.DMA((most_long,)),
+            pltpu.VMEM(cache.shape, BF),
+            pltpu.SMEM((tokens,), jnp.int32),
+            pltpu.SMEM((most_long,), jnp.int32),
+            pltpu.VMEM((tokens, QUERY_PER_KEY, SHORT_PAGES * PAGE_POSITIONS), F32),
+            pltpu.VMEM((most_long, QUERY_PER_KEY, (pages - SHORT_PAGES) * PAGE_POSITIONS), F32),
+            *[per_head] * 5,
+            *[per_long] * 3,
+            pltpu.SemaphoreType.DMA((1,)),
         ],
         compiler_params=pltpu.CompilerParams(vmem_limit_bytes=VMEM_LIMIT),
     )(lengths, table, proj, cosines, sines, sinks, cache)
 
 
 def expert_kernel(
-    att, wo_all, hidden, obias, egain, router, router_bias, routes, routes_t, w1_hbm, b1, w2_hbm, rbias,
+    att, wo_all, hidden, obias, egain, router, router_bias, routes_t, w1_hbm, b1, w2_hbm, rbias,
     out,
     w1, w2, heads, halves, summed, mine, outgoing, gathered, full, pre, near_out, near_in, far_out, far_in,
     kept, back_out, back_in, logits_out, logits_in, share_f32, gains,
@@ -480,10 +518,10 @@
     hot_t = jnp.zeros((count_req, tokens), F32)
     for k in range(routes_t.shape[0]):
         hot_t = hot_t + (routes_t[k : k + 1, :] == names).astype(F32)
-    names = lax.broadcasted_iota(jnp.int32, (tokens, count_req), 1)
-    hot = jnp.zeros((tokens, count_req), F32)
-    for k in range(routes.shape[1]):
-        hot = hot + (routes[:, k : k + 1] == names).astype(F32)
+    same = lax.broadcasted_iota(jnp.int32, (tokens, tokens), 0) == lax.broadcasted_iota(
+        jnp.int32, (tokens, tokens), 1
+    )
+    hot = dot_nt(same.astype(BF), hot_t.astype(BF))
     before = lax.broadcasted_iota(jnp.int32, (tokens, tokens), 0) < lax.broadcasted_iota(
         jnp.int32, (tokens, tokens), 1
     )
@@ -745,7 +783,7 @@
         remote(logits_out, logits_in.at[m], l_send.at[step], l_recv.at[step], r, to).wait_send()
 
 
-def experts(att, wo_all, hidden, obias, egain, router, router_bias, routes, routes_t, w1, b1, w2, rbias):
+def experts(att, wo_all, hidden, obias, egain, router, router_bias, routes_t, w1, b1, w2, rbias):
     tokens, width = hidden.shape
     count_req, count_mdl = NX * NZ, NY * NC
     share = width // count_mdl
@@ -761,7 +799,7 @@
         expert_kernel,
         name="experts",
         out_shape=jax.ShapeDtypeStruct((tokens, share), BF),
-        in_specs=[vmem] * 9 + [hbm, vmem, hbm, vmem],
+        in_specs=[vmem] * 8 + [hbm, vmem, hbm, vmem],
         out_specs=vmem,
         scratch_shapes=[
             pltpu.VMEM(w1.shape, BF),
@@ -799,7 +837,7 @@
         compiler_params=pltpu.CompilerParams(
             collective_id=2, has_side_effects=True, vmem_limit_bytes=VMEM_LIMIT
         ),
-    )(att, wo_all, hidden, obias, egain, router, router_bias, routes, routes_t, w1, b1, w2, rbias)
+    )(att, wo_all, hidden, obias, egain, router, router_bias, routes_t, w1, b1, w2, rbias)
 
 
 def rotation_tables(lengths, repeat):
@@ -837,11 +875,9 @@
     projected, wo_all = project(
         hidden_state, attention_gain[None], qkv_weight, output_weight.T, qkv_bias[None]
     )
-    pool = paged_cache_store.shape[0]
-    local_table = jnp.clip(page_table - lax.axis_index("req") * pool, 0, pool - 1)
     cosines, sines = rotation_tables(cached_length_list, 2)
     attended = attend(
-        cached_length_list, local_table, projected, cosines, sines, sink_logit_values[:, None], paged_cache_store
+        cached_length_list, page_table.T, projected, cosines, sines, sink_logit_values, paged_cache_store
     )
     return experts(
         attended,
@@ -851,7 +887,6 @@
         expert_gain[None],
         router_weight.T,
         router_bias[None],
-        expert_routes,
         expert_routes.T,
         expand_weight[0].T,
         expand_bias,

time: 139 us -> 120 us (0.86)
  Pallas kernels: 128 us -> 112 us
  local copies, waits for them, and re-layouts: 7.94 us -> 5.15 us
    pallas_call x1, Pallas kernels: 26.1 us -> 10.6 us  [attend(): pl.pallas_call(attend_kernel, name='attend', out_shape=jax.ShapeDtypeStru...]
    unnamed x9 -> x5, local copies, waits for them, and re-layouts: 2.82 us -> 1.36 us
where the time goes in v2:
time: 120 us; the launch traced here: 119 us
  Pallas kernels  112 us (93%)
  local copies, waits for them, and re-layouts  5.15 us (4%)
  other arithmetic  1.54 us (1%)
    pallas_call x1, Pallas kernels, experts(): pl.pallas_call(expert_kernel, name='experts', out_shape=jax.ShapeDtypeStr...  68.6 us
    pallas_call x1, Pallas kernels, project(): pl.pallas_call(project_kernel, name='project', out_shape=(jax.ShapeDtypeS...  33.3 us
    pallas_call x1, Pallas kernels, attend(): pl.pallas_call(attend_kernel, name='attend', out_shape=jax.ShapeDtypeStru...  10.6 us

profile of v2, /device:TPU:1, one launch (start us, length us, event | category | flops | bytes accessed | tf_op | source)
XLA Modules:
  0.0 119.1 jit_solution(15219749384714024531)
XLA Ops:
  0.0 0.0 copy-start
  0.0 0.0 copy-start.1
  0.0 0.7 convert_element_type.3
  0.7 0.1 fusion
  0.8 0.7 pad_maximum_fusion
  1.6 1.3 %broadcast_in_dim.17.gain = f32[1,2880]{1,0:T(1,128)} reshape(f32[2880]{0:T(1024)} %param.22) | data formatting | bytes 23040 | tf_op jit(solution)/shard_map/broadcast_in_dim | solution.py:876
  2.9 1.3 %broadcast_in_dim.18.bias = f32[1,640]{1,0:T(1,128)} reshape(f32[640]{0:T(1024)} %param.24) | data formatting | bytes 5120 | tf_op jit(solution)/shard_map/broadcast_in_dim | solution.py:876
  4.1 33.3 %project.1 = (f32[32,640]{1,0:T(8,128)}, bf16[8,90,512]{2,1,0:T(8,128)(2,1)}) custom-call(bf16[32,2880]{1,0:T(8,128)(2,1)} %hidden.3, f32[1,2880]{1,0:T(1,128)} %broadcast_in_dim.17.gain, bf16[90,640]{1,0:T(8,128)(2,1)} %wqkv.1, bf16[90,512]{1,0:T(8,128)(2,1)} %bitcast.12, f32[1,640]{1,0:T(1,128)} %broadcast_in_dim.18.bias), custom_call_target="tpu_custom_call" | custom-call | tf_op jit(solution)/shard_map/project/pallas_call | solution.py:253
  37.4 10.6 %attend.1.att = bf16[32,512]{1,0:T(8,128)(2,1)} custom-call(s32[32]{0:T(128)} %lengths.1, s32[16,32]{1,0:T(8,128)} %bitcast.13, f32[32,640]{1,0:T(8,128)} %get-tuple-element.7.proj, f32[32,128]{1,0:T(8,128)} %get-tuple-element.12.cosines, f32[32,128]{1,0:T(8,128)} %get-tuple-element.13.sines, f32[8]{0:T(128)} %sinks.1, bf16[176,128,128]{2,1,0:T(8,128)(2,1)} %cache.1), custom_call_target="tpu_custom_call" | custom-call | tf_op jit(solution)/shard_map/attend/pallas_call | solution.py:428
  48.0 0.0 copy-done
  48.0 0.6 broadcast_in_dim.19.obias
  48.6 0.0 copy-done.1
  48.6 0.6 broadcast_in_dim.20.egain
  49.2 68.6 %experts.1 = bf16[32,360]{1,0:T(8,128)(2,1)} custom-call(bf16[32,512]{1,0:T(8,128)(2,1)} %attend.1.att, bf16[8,90,512]{2,1,0:T(8,128)(2,1)} %get-tuple-element.8.wo_all, bf16[32,2880]{1,0:T(8,128)(2,1)} %hidden.3, f32[1,2880]{1,0:T(1,128)} %broadcast_in_dim.19.obias, f32[1,2880]{1,0:T(1,128)} %broadcast_in_dim.20.egain, bf16[32,2880]{1,0:T(8,128)(2,1)} %bitcast.11, ...), custom_call_target="tpu_custom_call" | custom-call | tf_op jit(solution)/shard_map/experts/pallas_call | solution.py:798
  117.8 1.3 %copy.20 = bf16[32,360]{1,0:T(8,128)(2,1)} copy(bf16[32,360]{1,0:T(8,128)(2,1)} %experts.1) | data formatting | bytes 46080
  (1 shorter events, 0.0 us)
Async XLA Ops:
  0.0 48.0 %copy-start = (f32[2880]{0:T(1024)S(1)}, f32[2880]{0:T(1024)}, u32[]{:S(2)}) copy-start(f32[2880]{0:T(1024)} %param.27) | copy-start | bytes 34564
  0.0 48.6 %copy-start.1 = (f32[2880]{0:T(1024)S(1)}, f32[2880]{0:T(1024)}, u32[]{:S(2)}) copy-start(f32[2880]{0:T(1024)} %param.28) | copy-start | bytes 34564

commit v3 on v2

--- a/solution.py
+++ b/solution.py
@@ -3,6 +3,7 @@
 
 import jax
 import jax.numpy as jnp
+import numpy as np
 from jax import lax
 from jax.experimental import pallas as pl
 from jax.experimental.pallas import tpu as pltpu
@@ -181,7 +182,7 @@
 
     value = hidden[...].astype(F32)
     scale = lax.rsqrt(jnp.mean(value * value, axis=-1, keepdims=True) + norm_epsilon)
-    normed = (value * scale * gain[...]).astype(BF)
+    normed = (value * scale * gain[...][None, :]).astype(BF)
     for k in range(NX):
         parcels[k] = normed[:, group * k : group * k + group]
 
@@ -228,7 +229,7 @@
         x_copy(sums, sums_in, s_send, s_recv, step).start()
     for way, dist, part in ring_o.plan:
         ring_o.step(way, dist, part)
-    result = total[x] + bias[...]
+    result = total[x] + bias[...][None, :]
     for step in range(1, NX):
         x_arrive(sums_in, s_send, s_recv, step)
         result = result + sums_in[(x + NX - step) % NX].astype(F32)
@@ -504,13 +505,14 @@
         remote(att, heads.at[x], x_send.at[step], x_recv.at[step], to * NZ + z, m).start()
     heads[x] = att[...]
 
+    obias_row, egain_row = obias[...][None, :], egain[...][None, :]
     for k in range(count_mdl):
 
         @pl.when(m == k)
         def _():
             at = slice(share * k, share * k + share)
-            share_f32[...] = hidden[:, at].astype(F32) + obias[:, at]
-            gains[0:1, :] = egain[:, at]
+            share_f32[...] = hidden[:, at].astype(F32) + obias_row[:, at]
+            gains[0:1, :] = egain_row[:, at]
             gains[8 : 8 + count_req, :] = rbias[:, at]
             gains[8 + count_req : 8 + 2 * count_req, :] = router[:, at].astype(F32)
 
@@ -842,14 +844,11 @@
 
 def rotation_tables(lengths, repeat):
     half = HEAD_SIZE // 2
-    exponent = jnp.arange(half, dtype=F32) * (2.0 / HEAD_SIZE)
-    frequency = jnp.power(rope_theta, -exponent)
+    frequency = np.power(rope_theta, -np.arange(half) * (2.0 / HEAD_SIZE))
+    frequency = np.tile(frequency, 2 * repeat).astype(np.float32)
+    sign = np.tile(np.repeat(np.float32([-1.0, 1.0]), half), repeat)
     angles = lengths.astype(F32)[:, None] * frequency[None, :]
-    cosine, sine = jnp.cos(angles), jnp.sin(angles)
-    return (
-        jnp.concatenate([cosine, cosine] * repeat, axis=1),
-        jnp.concatenate([-sine, sine] * repeat, axis=1),
-    )
+    return jnp.cos(angles), jnp.sin(angles) * sign[None, :]
 
 
 def shards(
@@ -873,7 +872,7 @@
     reduce_bias,
 ):
     projected, wo_all = project(
-        hidden_state, attention_gain[None], qkv_weight, output_weight.T, qkv_bias[None]
+        hidden_state, attention_gain, qkv_weight, output_weight.T, qkv_bias
     )
     cosines, sines = rotation_tables(cached_length_list, 2)
     attended = attend(
@@ -883,8 +882,8 @@
         attended,
         wo_all,
         hidden_state,
-        output_bias[None],
-        expert_gain[None],
+        output_bias,
+        expert_gain,
         router_weight.T,
         router_bias[None],
         expert_routes.T,

time: 120 us -> 116 us (0.967)
  local copies, waits for them, and re-layouts: 5.15 us -> 1.35 us
    broadcast_in_dim x4 -> x0, local copies, waits for them, and re-layouts: 3.8 us -> none  [the longest x1 1.31 us: shards(): attention_gain[None]]
    mul x0 -> x1, other arithmetic: none -> 1.43 us  [rotation_tables(): return (jnp.cos(angles), jnp.sin(angles) * sign[None, :])]
where the time goes in v3:
time: 116 us; the launch traced here: 115 us
  Pallas kernels  112 us (97%)
  other arithmetic  2.08 us (2%)
  local copies, waits for them, and re-layouts  1.35 us (1%)
    pallas_call x1, Pallas kernels, experts(): pl.pallas_call(expert_kernel, name='experts', out_shape=jax.ShapeDtypeStr...  67.9 us
    pallas_call x1, Pallas kernels, project(): pl.pallas_call(project_kernel, name='project', out_shape=(jax.ShapeDtypeS...  33.3 us
    pallas_call x1, Pallas kernels, attend(): pl.pallas_call(attend_kernel, name='attend', out_shape=jax.ShapeDtypeStru...  10.6 us

profile of v3, /device:TPU:1, one launch (start us, length us, event | category | flops | bytes accessed | tf_op | source)
XLA Modules:
  0.0 115.2 jit_solution(11672787902606565891)
XLA Ops:
  0.0 0.7 convert_element_type.3
  0.7 1.4 %fusion = (f32[32,128]{1,0:T(8,128)}, f32[32,128]{1,0:T(8,128)}) fusion(f32[128]{0:T(128)} %constant.13, f32[128]{0:T(128)} %constant.12, f32[32]{0:T(128)S(1)} %convert_element_type.3), kind=kLoop, calls=%fused_computation.2 | loop fusion | flops 8192 | bytes 33920 | tf_op jit(solution)/shard_map/mul | solution.py:851
  2.1 33.3 %project.1 = (f32[32,640]{1,0:T(8,128)}, bf16[8,90,512]{2,1,0:T(8,128)(2,1)}) custom-call(bf16[32,2880]{1,0:T(8,128)(2,1)} %hidden.3, f32[2880]{0:T(1024)} %gain.1, bf16[90,640]{1,0:T(8,128)(2,1)} %wqkv.1, bf16[90,512]{1,0:T(8,128)(2,1)} %bitcast.12, f32[640]{0:T(1024)} %bias.1), custom_call_target="tpu_custom_call" | custom-call | tf_op jit(solution)/shard_map/project/pallas_call | solution.py:254
  35.4 10.6 %attend.1.att = bf16[32,512]{1,0:T(8,128)(2,1)} custom-call(s32[32]{0:T(128)} %lengths.1, s32[16,32]{1,0:T(8,128)} %bitcast.13, f32[32,640]{1,0:T(8,128)} %get-tuple-element.7.proj, f32[32,128]{1,0:T(8,128)} %get-tuple-element.10.cosines, f32[32,128]{1,0:T(8,128)} %get-tuple-element.9.sines, f32[8]{0:T(128)} %sinks.1, bf16[176,128,128]{2,1,0:T(8,128)(2,1)} %cache.1), custom_call_target="tpu_custom_call" | custom-call | tf_op jit(solution)/shard_map/attend/pallas_call | solution.py:429
  46.0 67.9 %experts.1 = bf16[32,360]{1,0:T(8,128)(2,1)} custom-call(bf16[32,512]{1,0:T(8,128)(2,1)} %attend.1.att, bf16[8,90,512]{2,1,0:T(8,128)(2,1)} %get-tuple-element.8.wo_all, bf16[32,2880]{1,0:T(8,128)(2,1)} %hidden.3, f32[2880]{0:T(1024)} %obias.1, f32[2880]{0:T(1024)} %egain.1, bf16[32,2880]{1,0:T(8,128)(2,1)} %bitcast.11, f32[1,32]{1,0:T(1,128)} %bitcast.15, ...), custom_call_target="tpu_custom_call" | custom-call | tf_op jit(solution)/shard_map/experts/pallas_call | solution.py:800
  113.9 1.3 %copy.22 = bf16[32,360]{1,0:T(8,128)(2,1)} copy(bf16[32,360]{1,0:T(8,128)(2,1)} %experts.1) | data formatting | bytes 46080

commit v4 on v3

--- a/solution.py
+++ b/solution.py
@@ -355,12 +355,16 @@
 
     lax.fori_loop(0, count // at_once, score, 0)
 
-    def far_score(j, carry):
-        i = at_long[j]
-        far_scores[j] = masked(dot_nt(queries[i].astype(BF), entries(i, SHORT_PAGES, pages)), i, SHORT_MAX)
+    far_at_once = 4 if most_long % 4 == 0 else 1
+
+    def far_score(g, carry):
+        for u in range(far_at_once):
+            j = g * far_at_once + u
+            i = at_long[j]
+            far_scores[j] = masked(dot_nt(queries[i].astype(BF), entries(i, SHORT_PAGES, pages)), i, SHORT_MAX)
         return carry
 
-    lax.fori_loop(0, most_long, far_score, 0)
+    lax.fori_loop(0, most_long // far_at_once, far_score, 0)
 
     def weigh(held, tops, bottoms):
         raw = held[...]
@@ -381,11 +385,13 @@
 
     lax.fori_loop(0, count // at_once, mix, 0)
 
-    def far_mix(j, carry):
-        far_mixed[j] = dot(far_scores[j].astype(BF), entries(at_long[j], SHORT_PAGES, pages))
+    def far_mix(g, carry):
+        for u in range(far_at_once):
+            j = g * far_at_once + u
+            far_mixed[j] = dot(far_scores[j].astype(BF), entries(at_long[j], SHORT_PAGES, pages))
         return carry
 
-    lax.fori_loop(0, most_long, far_mix, 0)
+    lax.fori_loop(0, most_long // far_at_once, far_mix, 0)
 
     sink_rows = lax.broadcasted_iota(jnp.int32, (heads, channels), 0)
     sink = jnp.zeros((heads, channels), F32)

time: 116 us -> 114 us (0.983)
  Pallas kernels: 112 us -> 110 us
    pallas_call x1, Pallas kernels: 10.6 us -> 8.97 us  [attend(): pl.pallas_call(attend_kernel, name='attend', out_shape=jax.ShapeDtypeStru...]
where the time goes in v4:
time: 114 us
  Pallas kernels  110 us (96%)
  other arithmetic  2.08 us (2%)
  local copies, waits for them, and re-layouts  1.35 us (1%)
    pallas_call x1, Pallas kernels, experts(): pl.pallas_call(expert_kernel, name='experts', out_shape=jax.ShapeDtypeStr...  67.8 us
    pallas_call x1, Pallas kernels, project(): pl.pallas_call(project_kernel, name='project', out_shape=(jax.ShapeDtypeS...  33.3 us
    pallas_call x1, Pallas kernels, attend(): pl.pallas_call(attend_kernel, name='attend', out_shape=jax.ShapeDtypeStru...  8.97 us

profile of v4, /device:TPU:1, one launch (start us, length us, event | category | flops | bytes accessed | tf_op | source)
XLA Modules:
  0.0 113.5 jit_solution(17539741612222430960)
XLA Ops:
  0.0 0.7 convert_element_type.3
  0.7 1.4 %fusion = (f32[32,128]{1,0:T(8,128)}, f32[32,128]{1,0:T(8,128)}) fusion(f32[128]{0:T(128)} %constant.13, f32[128]{0:T(128)} %constant.12, f32[32]{0:T(128)S(1)} %convert_element_type.3), kind=kLoop, calls=%fused_computation.2 | loop fusion | flops 8192 | bytes 33920 | tf_op jit(solution)/shard_map/mul | solution.py:857
  2.1 33.3 %project.1 = (f32[32,640]{1,0:T(8,128)}, bf16[8,90,512]{2,1,0:T(8,128)(2,1)}) custom-call(bf16[32,2880]{1,0:T(8,128)(2,1)} %hidden.3, f32[2880]{0:T(1024)} %gain.1, bf16[90,640]{1,0:T(8,128)(2,1)} %wqkv.1, bf16[90,512]{1,0:T(8,128)(2,1)} %bitcast.12, f32[640]{0:T(1024)} %bias.1), custom_call_target="tpu_custom_call" | custom-call | tf_op jit(solution)/shard_map/project/pallas_call | solution.py:254
  35.4 9.0 %attend.1.att = bf16[32,512]{1,0:T(8,128)(2,1)} custom-call(s32[32]{0:T(128)} %lengths.1, s32[16,32]{1,0:T(8,128)} %bitcast.13, f32[32,640]{1,0:T(8,128)} %get-tuple-element.7.proj, f32[32,128]{1,0:T(8,128)} %get-tuple-element.10.cosines, f32[32,128]{1,0:T(8,128)} %get-tuple-element.9.sines, f32[8]{0:T(128)} %sinks.1, bf16[176,128,128]{2,1,0:T(8,128)(2,1)} %cache.1), custom_call_target="tpu_custom_call" | custom-call | tf_op jit(solution)/shard_map/attend/pallas_call | solution.py:435
  44.4 67.8 %experts.1 = bf16[32,360]{1,0:T(8,128)(2,1)} custom-call(bf16[32,512]{1,0:T(8,128)(2,1)} %attend.1.att, bf16[8,90,512]{2,1,0:T(8,128)(2,1)} %get-tuple-element.8.wo_all, bf16[32,2880]{1,0:T(8,128)(2,1)} %hidden.3, f32[2880]{0:T(1024)} %obias.1, f32[2880]{0:T(1024)} %egain.1, bf16[32,2880]{1,0:T(8,128)(2,1)} %bitcast.11, f32[1,32]{1,0:T(1,128)} %bitcast.15, ...), custom_call_target="tpu_custom_call" | custom-call | tf_op jit(solution)/shard_map/experts/pallas_call | solution.py:806
  112.2 1.3 %copy.22 = bf16[32,360]{1,0:T(8,128)(2,1)} copy(bf16[32,360]{1,0:T(8,128)(2,1)} %experts.1) | data formatting | bytes 46080
